TPU v7x, 8 devices: a whole 2x2x1 slice. The times are simulated.
8 devices in a mesh: prompts: 1 (over z), model: 2 (over y), resp: 4 (over x, core).
Axes of the slice: x: 2, y: 2, z: 1, core: 2. Of those that a mesh axis runs over, the one named last changes fastest.
Arguments:
- x_prompt: bfloat16 [512, 1536], P(('prompts', 'resp'))
- x_resp: bfloat16 [4, 1024, 1536], P(('prompts', 'resp'))
- targets: int32 [4, 1024], P(('prompts', 'resp'))
- attn_norm: float32 [2, 1536], replicated
- mlp_norm: float32 [2, 1536], replicated
- w_q: bfloat16 [2, 1536, 12, 128], P(None, None, 'model')
- w_k: bfloat16 [2, 1536, 2, 128], P(None, None, 'model')
- w_v: bfloat16 [2, 1536, 2, 128], P(None, None, 'model')
- w_o: bfloat16 [2, 12, 128, 1536], P(None, 'model')
- w_gate: bfloat16 [2, 1536, 8960], P(None, None, 'model')
- w_up: bfloat16 [2, 1536, 8960], P(None, None, 'model')
- w_down: bfloat16 [2, 8960, 1536], P(None, 'model')
- final_norm: float32 [1536], replicated
- w_head: bfloat16 [1536, 8192], P(None, 'model')
Outputs:
- output: float32 [4, 1024], P(('prompts', 'resp'))
All inputs are finite; a program needn't handle non-finite values.
Results may differ from a plain program's by a relative error of at most 0.00308508.
Values are sent between devices in bfloat16 or wider.
A program may use at most 1 GiB of HBM per device.

v0:
```python
import math
import jax
import jax.numpy as jnp
from jax import lax
from jax.sharding import PartitionSpec as P

RMS_EPS = 1e-6
ROPE_BASE = 10000.0
NEG_BIG = -1e30


def rms_norm(x_in, norm_gain):
    x_f = x_in.astype(jnp.float32)
    mean_sq = jnp.mean(x_f * x_f, axis=-1, keepdims=True)
    return (x_f * lax.rsqrt(mean_sq + RMS_EPS) * norm_gain).astype(jnp.bfloat16)


def rope_tables(positions, head_dim):
    inv_freq = jnp.exp(jnp.arange(0, head_dim, 2, dtype=jnp.float32) * (-math.log(ROPE_BASE) / head_dim))
    angles = positions.astype(jnp.float32)[:, None] * inv_freq[None, :]
    return jnp.cos(angles), jnp.sin(angles)


def apply_rope(proj_f, cos_tab, sin_tab):
    half_dim = proj_f.shape[-1] // 2
    lo_half = proj_f[..., :half_dim]
    hi_half = proj_f[..., half_dim:]
    cos_b = cos_tab[:, None, :]
    sin_b = sin_tab[:, None, :]
    return jnp.concatenate([lo_half * cos_b - hi_half * sin_b, hi_half * cos_b + lo_half * sin_b], axis=-1)


def heads_proj(hidden, w_mat):
    return jnp.einsum('td,dhe->the', hidden, w_mat, preferred_element_type=jnp.float32)


def attend_local(queries, key_rows, val_rows, q_pos, k_pos):
    q_len, heads_loc, head_dim = queries.shape
    kv_loc = key_rows.shape[1]
    q_grp = queries.reshape(q_len, kv_loc, heads_loc // kv_loc, head_dim)
    scores = jnp.einsum('qhre,khe->hrqk', q_grp, key_rows, preferred_element_type=jnp.float32) * (1.0 / math.sqrt(head_dim))
    scores = jnp.where(k_pos[None, :] <= q_pos[:, None], scores, NEG_BIG)
    attn_probs = jax.nn.softmax(scores, axis=-1).astype(jnp.bfloat16)
    attn_mix = jnp.einsum('hrqk,khe->qhre', attn_probs, val_rows, preferred_element_type=jnp.float32)
    return attn_mix.astype(jnp.bfloat16).reshape(q_len, heads_loc, head_dim)


def finish_layer(x_in, attn_mix, w_out, gain_mlp, w_gate_l, w_up_l, w_down_l):
    attn_proj = lax.psum(jnp.einsum('the,hed->td', attn_mix, w_out, preferred_element_type=jnp.float32), 'model')
    x_mid = (x_in.astype(jnp.float32) + attn_proj).astype(jnp.bfloat16)
    hidden = rms_norm(x_mid, gain_mlp)
    gate_proj = jnp.dot(hidden, w_gate_l, preferred_element_type=jnp.float32)
    up_proj = jnp.dot(hidden, w_up_l, preferred_element_type=jnp.float32)
    act_vals = (jax.nn.silu(gate_proj) * up_proj).astype(jnp.bfloat16)
    down_proj = lax.psum(jnp.dot(act_vals, w_down_l, preferred_element_type=jnp.float32), 'model')
    return (x_mid.astype(jnp.float32) + down_proj).astype(jnp.bfloat16)


def token_logp(x_res, final_norm, w_head_loc, tgt_row, model_idx):
    logits = jnp.dot(rms_norm(x_res, final_norm), w_head_loc, preferred_element_type=jnp.float32)
    vocab_loc = logits.shape[1]
    top_val = lax.pmax(jnp.max(logits, axis=-1), 'model')
    exp_sum = jnp.sum(jnp.exp(logits - top_val[:, None]), axis=-1)
    vocab_ids = model_idx * vocab_loc + jnp.arange(vocab_loc)
    picked = jnp.sum(jnp.where(vocab_ids[None, :] == tgt_row[:, None], logits, 0.0), axis=-1)
    totals = lax.psum(jnp.stack([exp_sum, picked]), 'model')
    return totals[1] - top_val - jnp.log(totals[0])


def solution(mesh):
    group_size = mesh.shape['resp']
    rows_spec = P(('prompts', 'resp'), None)
    in_specs = (rows_spec, P(('prompts', 'resp'), None, None), rows_spec, P(), P(),
                P(None, None, 'model', None), P(None, None, 'model', None), P(None, None, 'model', None),
                P(None, 'model', None, None), P(None, None, 'model'), P(None, None, 'model'),
                P(None, 'model', None), P(), P(None, 'model'))

    def local_pass(x_piece, x_own, tgt_own, attn_norm, mlp_norm, w_q, w_k, w_v, w_o, w_gate, w_up, w_down, final_norm, w_head):
        piece_len = x_piece.shape[0]
        resp_len = x_own.shape[1]
        head_dim = w_q.shape[3]
        prompt_len = piece_len * group_size
        dev_idx = lax.axis_index('resp')
        model_idx = lax.axis_index('model')
        piece_pos = dev_idx * piece_len + jnp.arange(piece_len)
        resp_pos = prompt_len + jnp.arange(resp_len)
        tok_pos = jnp.concatenate([piece_pos, resp_pos])
        key_pos = jnp.concatenate([jnp.arange(prompt_len), resp_pos])
        tok_cos, tok_sin = rope_tables(tok_pos, head_dim)
        x_tok = jnp.concatenate([x_piece, x_own[0]], axis=0)

        hidden = rms_norm(x_tok, attn_norm[0])
        q_tok = apply_rope(heads_proj(hidden, w_q[0]), tok_cos, tok_sin).astype(jnp.bfloat16)
        k_tok = apply_rope(heads_proj(hidden, w_k[0]), tok_cos, tok_sin).astype(jnp.bfloat16)
        v_tok = heads_proj(hidden, w_v[0]).astype(jnp.bfloat16)
        kv_prompt = lax.all_gather(jnp.stack([k_tok[:piece_len], v_tok[:piece_len]]), 'resp', axis=1, tiled=True)
        key_rows = jnp.concatenate([kv_prompt[0], k_tok[piece_len:]], axis=0)
        val_rows = jnp.concatenate([kv_prompt[1], v_tok[piece_len:]], axis=0)
        attn_mix = attend_local(q_tok, key_rows, val_rows, tok_pos, key_pos)
        x_tok = finish_layer(x_tok, attn_mix, w_o[0], mlp_norm[0], w_gate[0], w_up[0], w_down[0])

        hidden = rms_norm(x_tok, attn_norm[1])
        k_tok = apply_rope(heads_proj(hidden, w_k[1]), tok_cos, tok_sin).astype(jnp.bfloat16)
        v_tok = heads_proj(hidden, w_v[1]).astype(jnp.bfloat16)
        q_own = apply_rope(heads_proj(hidden[piece_len:], w_q[1]), tok_cos[piece_len:], tok_sin[piece_len:]).astype(jnp.bfloat16)
        kv_prompt = lax.all_gather(jnp.stack([k_tok[:piece_len], v_tok[:piece_len]]), 'resp', axis=1, tiled=True)
        key_rows = jnp.concatenate([kv_prompt[0], k_tok[piece_len:]], axis=0)
        val_rows = jnp.concatenate([kv_prompt[1], v_tok[piece_len:]], axis=0)
        attn_mix = attend_local(q_own, key_rows, val_rows, resp_pos, key_pos)
        x_res = finish_layer(x_tok[piece_len:], attn_mix, w_o[1], mlp_norm[1], w_gate[1], w_up[1], w_down[1])
        return token_logp(x_res, final_norm, w_head, tgt_own[0], model_idx)[None, :]

    return jax.shard_map(local_pass, mesh=mesh, in_specs=in_specs, out_specs=rows_spec, check_vma=False)
```

profile of v0, /device:TPU:0, one launch (start us, length us, event | category | flops | bytes accessed | tf_op | source)
XLA Modules:
  0.0 1010.0 jit_solution(2007165018709740466)
XLA Ops:
  6.6 2.8 fusion.36
  10.8 2.9 fusion.38
  24.0 11.0 %all_gather.6 = bf16[2,512,1,128]{1,3,2,0:T(8,128)(2,1)S(1)} all-gather(bf16[2,128,1,128]{1,3,2,0:T(8,128)(2,1)S(1)} %pad_maximum_fusion.1), channel_id=1, replica_groups=mesh['prompts'=1,'model'=2,'resp'=4] {'resp'}, dimensions={1}, use_global_device_ids=true | all-gather | bytes 327680 | tf_op jit(solution)/shard_map/all_gather | solution.py:96
  35.7 4.8 fusion.164
  40.6 4.3 copy.39
  44.9 5.0 fusion.168
  51.7 17.7 %fusion.166 = (f32[6,1152]{1,0:T(8,128)}, f32[1,6,1152,1536]{2,3,1,0:T(8,128)}) fusion(bf16[1152,6,64]{0,2,1:T(8,128)(2,1)S(1)} %get-tuple-element.20, bf16[1152,6,64]{0,2,1:T(8,128)(2,1)S(1)} %get-tuple-element.19, bf16[1152,1,64]{0,2,1:T(8,128)(2,1)} %copy-done.20, bf16[1152,1,64]{0,2,1:T(8,128)(2,1)} %copy-done.19, ...), kind=kOutput, calls=%fused_computation.199 | convolution fusion | flops 2755060992 | bytes 46459904 | tf_op jit(solution)/shard_map/qhre,khe->hrqk/dot_general | solution.py:41
  69.5 16.5 %fusion = f32[6,1152]{1,0:T(8,128)S(1)} fusion(f32[1,6,1152,1536]{2,3,1,0:T(8,128)} %get-tuple-element.38, f32[6,1152]{1,0:T(8,128)} %get-tuple-element.37), kind=kLoop, calls=%fused_computation.6 | loop fusion | flops 21226752 | bytes 42522624 | tf_op jit(solution)/shard_map/reduce_sum | solution.py:43
  86.0 21.1 %convolution_bitcast_fusion = f32[1152,1536]{1,0:T(8,128)} fusion(bf16[2,6,128,1536]{3,2,1,0:T(8,128)(2,1)} %param.22, f32[6,1152]{1,0:T(8,128)S(1)} %fusion, f32[1,6,1152,1536]{2,3,1,0:T(8,128)} %get-tuple-element.38, f32[6,1152]{1,0:T(8,128)S(1)} %copy-done.29, bf16[1024,1,128]{0,2,1:T(8,128)(2,1)S(1)} %copy-done.21, bf16[512,1,128]{0,2,1:T(8,128)(2,1)S(1)} %copy-done.24), kind=kOutput, calls=%fused_computation.47 | convolution fusion | flops 5469339648 | bytes 52353024 | tf_op jit(solution)/shard_map/the,hed->td/dot_general | solution.py:49
  108.4 163.3 %all-reduce.5.cloned.1.call-done = f32[1152,1536]{1,0:T(8,128)} async-done(((f32[1152,1536]{1,0:T(8,128)}), f32[1152,1536]{1,0:T(8,128)}) %all-reduce.5.cloned.1.call-update) | async-done | bytes 7077904 | tf_op jit(solution)/shard_map/psum | solution.py:49
  271.6 3.7 fusion.40
  277.1 22.5 %fusion.19 = f32[1152,4480]{1,0:T(8,128)} fusion(bf16[2,1536,4480]{2,1,0:T(8,128)(2,1)} %param.23, bf16[1152,1536]{1,0:T(8,128)(2,1)S(1)} %get-tuple-element.16, f32[1536]{0:T(1024)S(1)} %copy-done.34, f32[1152]{0:T(1024)S(1)} %add_rsqrt_fusion.1), kind=kOutput, calls=%fused_computation.27 | convolution fusion | flops 15861547008 | bytes 37956096 | tf_op jit(solution)/shard_map/dot_general | solution.py:52
  299.6 26.7 %fusion.5.clone.5 = bf16[1152,4480]{1,0:T(8,128)(2,1)} fusion(f32[1152,4480]{1,0:T(8,128)} %fusion.19, bf16[2,1536,4480]{2,1,0:T(8,128)(2,1)} %param.24, bf16[1152,1536]{1,0:T(8,128)(2,1)} %copy-done.1, f32[1536]{0:T(1024)S(1)} %copy-done.34, f32[1152]{0:T(1024)S(1)} %add_rsqrt_fusion.1), kind=kOutput, calls=%fused_computation.12.clone.clone.clone.2 | convolution fusion | flops 15892512768 | bytes 48278016 | tf_op jit(solution)/shard_map/dot_general | solution.py:53
  326.4 23.9 %fusion.14 = f32[1152,1536]{1,0:T(8,128)} fusion(bf16[2,4480,1536]{2,1,0:T(8,128)(2,1)} %param.25, bf16[1152,4480]{1,0:T(8,128)(2,1)} %fusion.5.clone.5), kind=kOutput, calls=%fused_computation.24 | convolution fusion | flops 15854469120 | bytes 31162368 | tf_op jit(solution)/shard_map/dot_general | solution.py:55
  357.2 157.6 %all-reduce.7.cloned.1.call-done = f32[1152,1536]{1,0:T(8,128)} async-done(((f32[1152,1536]{1,0:T(8,128)}), f32[1152,1536]{1,0:T(8,128)}) %all-reduce.7.cloned.1.call-update) | async-done | bytes 7077904 | tf_op jit(solution)/shard_map/psum | solution.py:55
  514.8 5.1 fusion.33
  525.6 8.9 all_gather.7
  535.2 2.6 fusion.56
  539.3 16.5 %fusion.2 = (f32[6,1024]{1,0:T(8,128)S(1)}, f32[1536,1024,6]{1,0,2:T(8,128)}) fusion(pred[1024,1536]{0,1:T(8,128)(4,1)S(1)} %copy-done.5, bf16[1024,6,64]{0,2,1:T(8,128)(2,1)} %get-tuple-element.22, bf16[1024,6,64]{0,2,1:T(8,128)(2,1)S(1)} %get-tuple-element.21, bf16[1152,1,64]{0,2,1:T(8,128)(2,1)S(1)} %get-tuple-element.24, ...), kind=kOutput, calls=%fused_computation.8 | convolution fusion | flops 2449139712 | bytes 41345024 | tf_op jit(solution)/shard_map/qhre,khe->hrqk/dot_general | solution.py:41
  555.8 17.1 %fusion.1 = f32[6,1024]{1,0:T(8,128)} fusion(f32[1536,1024,6]{1,0,2:T(8,128)} %get-tuple-element.40, f32[6,1024]{1,0:T(8,128)S(1)} %get-tuple-element.39, pred[1024,1536]{0,1:T(8,128)(4,1)S(1)} %copy-done.5), kind=kLoop, calls=%fused_computation.7 | loop fusion | flops 37742592 | bytes 39370752 | tf_op jit(solution)/shard_map/reduce_sum | solution.py:43
  572.9 20.6 %convolution_bitcast_fusion.1 = f32[1024,1536]{1,0:T(8,128)} fusion(bf16[2,6,128,1536]{3,2,1,0:T(8,128)(2,1)} %param.22, f32[6,1024]{1,0:T(8,128)} %fusion.1, f32[6,1024]{1,0:T(8,128)} %copy-done.30, f32[1536,1024,6]{1,0,2:T(8,128)} %get-tuple-element.40, pred[1024,1536]{0,1:T(8,128)(4,1)} %broadcast_compare_fusion.1, ...), kind=kOutput, calls=%fused_computation.69 | convolution fusion | flops 4880596992 | bytes 48431104 | tf_op jit(solution)/shard_map/the,hed->td/dot_general | solution.py:49
  593.8 146.3 %all-reduce.9.cloned.1.call-done = f32[1024,1536]{1,0:T(8,128)} async-done(((f32[1024,1536]{1,0:T(8,128)}), f32[1024,1536]{1,0:T(8,128)}) %all-reduce.9.cloned.1.call-update) | async-done | bytes 6291472 | tf_op jit(solution)/shard_map/psum | solution.py:49
  740.1 3.8 fusion.47
  743.9 21.4 %fusion.10 = f32[1024,4480]{1,0:T(8,128)} fusion(bf16[2,1536,4480]{2,1,0:T(8,128)(2,1)} %param.24, bf16[1024,1536]{1,0:T(8,128)(2,1)S(1)} %get-tuple-element.12, f32[1536]{0:T(1024)S(1)} %copy-done.33, f32[1024]{0:T(1024)S(1)} %add_rsqrt_fusion.4), kind=kOutput, calls=%fused_computation.20 | convolution fusion | flops 14099152896 | bytes 35268608 | tf_op jit(solution)/shard_map/dot_general | solution.py:53
  765.4 25.3 %multiply_convert_fusion.5 = bf16[1024,4480]{1,0:T(8,128)(2,1)} fusion(f32[1024,4480]{1,0:T(8,128)} %fusion.10, bf16[2,1536,4480]{2,1,0:T(8,128)(2,1)} %param.23, bf16[1024,1536]{1,0:T(8,128)(2,1)S(1)} %get-tuple-element.12, f32[1536]{0:T(1024)S(1)} %copy-done.33, f32[1024]{0:T(1024)S(1)} %add_rsqrt_fusion.4), kind=kOutput, calls=%fused_computation.15.clone.clone.2 | convolution fusion | flops 14126678016 | bytes 44443648 | tf_op jit(solution)/shard_map/dot_general | solution.py:52
  790.6 21.5 %fusion.8 = f32[1024,1536]{1,0:T(8,128)} fusion(bf16[2,4480,1536]{2,1,0:T(8,128)(2,1)} %param.25, bf16[1024,4480]{1,0:T(8,128)(2,1)} %multiply_convert_fusion.5), kind=kOutput, calls=%fused_computation.18 | convolution fusion | flops 14092861440 | bytes 29229056 | tf_op jit(solution)/shard_map/dot_general | solution.py:55
  812.2 147.5 %all-reduce.11.cloned.1.call-done = f32[1024,1536]{1,0:T(8,128)} async-done(((f32[1024,1536]{1,0:T(8,128)}), f32[1024,1536]{1,0:T(8,128)}) %all-reduce.11.cloned.1.call-update) | async-done | bytes 6291472 | tf_op jit(solution)/shard_map/psum | solution.py:55
  959.7 3.8 fusion.44
  964.3 20.0 %fusion.167 = (f32[1024]{0:T(1024)S(1)}, f32[1024,4096]{1,0:T(8,128)}) fusion(bf16[1536,4096]{1,0:T(8,128)(2,1)} %param.27, f32[1536]{0:T(1024)S(1)} %copy-done.38, f32[1024]{0:T(1024)S(1)} %add_rsqrt_fusion.3, f32[1024,1536]{1,0:T(8,128)S(1)} %copy-done.6, bf16[1024,1536]{1,0:T(8,128)(2,1)S(1)} %copy-done.3), kind=kOutput, calls=%fused_computation.200 | convolution fusion | flops 12900105216 | bytes 38811648 | tf_op jit(solution)/shard_map/dot_general | solution.py:60
  984.3 4.9 pmax.7
  989.2 8.2 exponential_reduce_fusion
  997.4 5.0 psum.39
  (128 shorter events, 33.7 us)
Async XLA Ops:
  6.5 265.1 %all-reduce.5.cloned.1.call-start = ((), (), s32[]{:S(2)}) async-start(), calls=%async_computation | async-start | bytes 14155776 | tf_op jit(solution)/shard_map/psum | solution.py:49
  6.5 7.1 copy-start.17
  6.5 43.3 %copy-start.27 = (s32[1024]{0:T(1024)}, s32[1024]{0:T(1024)S(1)}, u32[]{:S(2)}) copy-start(s32[1024]{0:T(1024)S(1)} %iota_add_fusion.1) | copy-start | bytes 12292
  6.6 13.7 %copy-start.35 = (f32[64]{0:T(128)}, f32[64]{0:T(128)S(1)}, u32[]{:S(2)}) copy-start(f32[64]{0:T(128)S(1)} %multiply_exponential_fusion) | copy-start | bytes 772
  9.3 6.9 copy-start.15
  18.3 4.2 copy-start.22
  44.9 6.3 copy-start.8
  44.9 6.4 copy-start.10
  69.5 16.5 %copy-start.21 = (bf16[1024,1,128]{0,2,1:T(8,128)(2,1)S(1)}, bf16[1024,1,128]{0,2,1:T(8,128)(2,1)}, u32[]{:S(2)}) copy-start(bf16[1024,1,128]{0,2,1:T(8,128)(2,1)} %slice_bitcast_fusion.1) | copy-start | bytes 786436
  69.5 16.5 %copy-start.24 = (bf16[512,1,128]{0,2,1:T(8,128)(2,1)S(1)}, bf16[512,1,128]{0,2,1:T(8,128)(2,1)}, u32[]{:S(2)}) copy-start(bf16[512,1,128]{0,2,1:T(8,128)(2,1)} %get-tuple-element.29) | copy-start | bytes 393220
  69.5 16.5 %copy-start.29 = (f32[6,1152]{1,0:T(8,128)S(1)}, f32[6,1152]{1,0:T(8,128)}, u32[]{:S(2)}) copy-start(f32[6,1152]{1,0:T(8,128)} %get-tuple-element.37) | copy-start | bytes 82948
  107.0 164.6 %copy-start = (bf16[1,1024,1536]{2,1,0:T(8,128)(2,1)S(1)}, bf16[1,1024,1536]{2,1,0:T(8,128)(2,1)}, u32[]{:S(2)}) copy-start(bf16[1,1024,1536]{2,1,0:T(8,128)(2,1)} %param.15) | copy-start | bytes 9437188
  107.0 164.6 %copy-start.7 = (bf16[128,1536]{1,0:T(8,128)(2,1)S(1)}, bf16[128,1536]{1,0:T(8,128)(2,1)}, u32[]{:S(2)}) copy-start(bf16[128,1536]{1,0:T(8,128)(2,1)} %param.14) | copy-start | bytes 1179652
  107.1 407.7 %all-reduce.7.cloned.1.call-start = ((), (), s32[]{:S(2)}) async-start(), calls=%async_computation.1 | async-start | bytes 14155776 | tf_op jit(solution)/shard_map/psum | solution.py:55
  108.4 168.8 %copy-start.34 = (f32[1536]{0:T(1024)S(1)}, f32[1536]{0:T(1024)}, u32[]{:S(2)}) copy-start(f32[1536]{0:T(1024)} %get-tuple-element.8) | copy-start | bytes 18436
  350.3 4.9 copy-start.26
  350.3 4.9 copy-start.28
  350.3 389.8 %all-reduce.9.cloned.1.call-start = ((), (), s32[]{:S(2)}) async-start(), calls=%async_computation.2 | async-start | bytes 12582912 | tf_op jit(solution)/shard_map/psum | solution.py:49
  357.2 162.8 %copy-start.31 = (f32[1536]{0:T(1024)S(1)}, f32[1536]{0:T(1024)}, u32[]{:S(2)}) copy-start(f32[1536]{0:T(1024)} %get-tuple-element.9) | copy-start | bytes 18436
  521.1 3.2 copy-start.23
  521.1 3.2 copy-start.36
  521.1 14.2 %copy-start.12 = (bf16[1,1536,6,128]{1,3,2,0:T(8,128)(2,1)S(1)}, bf16[1,1536,6,128]{1,3,2,0:T(8,128)(2,1)}, u32[]{:S(2)}) copy-start(bf16[1,1536,6,128]{1,3,2,0:T(8,128)(2,1)} %copy.40) | copy-start | bytes 7077892
  535.2 2.7 copy-start.14
  535.2 4.1 copy-start.5
  555.8 17.1 %copy-start.30 = (f32[6,1024]{1,0:T(8,128)}, f32[6,1024]{1,0:T(8,128)S(1)}, u32[]{:S(2)}) copy-start(f32[6,1024]{1,0:T(8,128)S(1)} %get-tuple-element.39) | copy-start | bytes 73732
  593.5 150.4 %copy-start.33 = (f32[1536]{0:T(1024)S(1)}, f32[1536]{0:T(1024)}, u32[]{:S(2)}) copy-start(f32[1536]{0:T(1024)} %get-tuple-element.7) | copy-start | bytes 18436
  593.5 366.1 %all-reduce.11.cloned.1.call-start = ((), (), s32[]{:S(2)}) async-start(), calls=%async_computation.3 | async-start | bytes 12582912 | tf_op jit(solution)/shard_map/psum | solution.py:55
  743.9 21.4 %copy-start.2 = (bf16[1024,1536]{1,0:T(8,128)(2,1)}, bf16[1024,1536]{1,0:T(8,128)(2,1)S(1)}, u32[]{:S(2)}) copy-start(bf16[1024,1536]{1,0:T(8,128)(2,1)S(1)} %get-tuple-element.12) | copy-start | bytes 9437188
  812.1 147.6 %copy-start.3 = (bf16[1024,1536]{1,0:T(8,128)(2,1)S(1)}, bf16[1024,1536]{1,0:T(8,128)(2,1)}, u32[]{:S(2)}) copy-start(bf16[1024,1536]{1,0:T(8,128)(2,1)} %copy-done.2) | copy-start | bytes 9437188
  812.2 151.4 %copy-start.38 = (f32[1536]{0:T(1024)S(1)}, f32[1536]{0:T(1024)}, u32[]{:S(2)}) copy-start(f32[1536]{0:T(1024)} %param.26) | copy-start | bytes 18436
  959.7 4.6 copy-start.6
  964.3 24.9 %copy-start.37 = (s32[1,1024]{1,0:T(1,128)S(1)}, s32[1,1024]{1,0:T(1,128)}, u32[]{:S(2)}) copy-start(s32[1,1024]{1,0:T(1,128)} %param.16) | copy-start | bytes 12292
  (11 other events, 16.3 us)
Sparse Core Ops, SparseCore 0:
  107.2 164.3 all-reduce.4
  350.4 164.3 all-reduce.6
  593.7 146.4 all-reduce.8
  812.3 147.3 all-reduce.10
where the time goes:
time: 1010 us
  waiting for transfers between devices  615 us (61%)
  matrix products  250 us (25%)
  other arithmetic  76.9 us (8%)
  blocking collectives  29.9 us (3%)
  local copies, waits for them, and re-layouts  23 us (2%)
  between operations  14 us (1%)
    psum x2, waiting for transfers between devices, finish_layer(): lax.psum(jnp.einsum('the,hed->td', attn_mix, w_out, preferred_element_typ...  310 us
    psum x2, waiting for transfers between devices, finish_layer(): lax.psum(jnp.dot(act_vals, w_down_l, preferred_element_type=jnp.float32),...  305 us
    dot_general x2, matrix products, finish_layer(): up_proj = jnp.dot(hidden, w_up_l, preferred_element_type=jnp.float32)  48.1 us
    dot_general x2, matrix products, finish_layer(): gate_proj = jnp.dot(hidden, w_gate_l, preferred_element_type=jnp.float32)  47.8 us
    dot_general x2, matrix products, finish_layer(): jnp.dot(act_vals, w_down_l, preferred_element_type=jnp.float32)  45.4 us
    dot_general x2, matrix products, finish_layer(): jnp.einsum('the,hed->td', attn_mix, w_out, preferred_element_type=jnp.flo...  41.6 us
    dot_general x2, matrix products, attend_local(): jnp.einsum('qhre,khe->hrqk', q_grp, key_rows, preferred_element_type=jnp....  34.2 us
    reduce_sum x2, other arithmetic, attend_local(): attn_probs = jax.nn.softmax(scores, axis=-1).astype(jnp.bfloat16)  33.6 us
  transfers between devices with their start and end apart: 4, of which 4 were waited for; matrix products, arithmetic and copies ran while one was open for 1% of the time, Pallas kernels for 0%

commit v1 on v0

v1 whole, which is shorter than its diff:
```python
import functools
import math
import jax
import jax.numpy as jnp
from jax import lax
from jax.experimental import pallas as pl
from jax.experimental.pallas import tpu as pltpu
from jax.sharding import PartitionSpec as P

RMS_EPS = 1e-6
ROPE_BASE = 10000.0
NEG_BIG = -1e30
LOG2E = 1.4426950408889634
CHUNKS = (2, 3, 3)
FF_BLOCK = 768
HEAD_BLOCK = 1024
ATTN_MIB, MLP_MIB, HEAD_MIB = 40, 60, 60
bf16, f32 = jnp.bfloat16, jnp.float32


def normed(x_in, gain):
    x_f = x_in.astype(f32)
    mean_sq = jnp.mean(x_f * x_f, axis=-1, keepdims=True)
    return (x_f * lax.rsqrt(mean_sq + RMS_EPS) * gain).astype(bf16)


def mm(a, b):
    return jnp.dot(a, b, preferred_element_type=f32)


def whole(shape):
    return pl.BlockSpec(shape, lambda *_: (0,) * len(shape), pipeline_mode=pl.Buffered(1))


ORDER_ONLY = pl.BlockSpec(memory_space=pl.ANY)


def call(body, name, flops, mib, grid, in_specs, out_shape, scratch, args, after):
    n_in, n_after = len(args), len(after)

    def run(*refs):
        body(*refs[:n_in], *refs[n_in + n_after:])

    return pl.pallas_call(
        run, name=name, grid=grid,
        in_specs=list(in_specs) + [ORDER_ONLY] * n_after,
        out_specs=[whole(o.shape) for o in out_shape], out_shape=out_shape, scratch_shapes=scratch,
        cost_estimate=pl.CostEstimate(flops=int(flops), bytes_accessed=0, transcendentals=0),
        compiler_params=pltpu.CompilerParams(vmem_limit_bytes=mib << 20),
    )(*args, *after)


def rotate(z, cos, sin):
    return (z * cos + pltpu.roll(z, z.shape[1] // 2, 1) * sin).astype(bf16)


def swapped(x, half):
    model = lax.axis_index('model')
    return x + jnp.where(x < half, (1 - model) * half, (model - 1) * half)


def causal(rows):
    q = swapped(lax.broadcasted_iota(jnp.int32, (rows, rows), 0), rows // 2)
    k = swapped(lax.broadcasted_iota(jnp.int32, (rows, rows), 1), rows // 2)
    return jnp.where(k <= q, 0.0, NEG_BIG)


def x_halves(xs, at, half):
    if at is None:
        model = lax.axis_index('model')
        pick = lambda side: [x[pl.ds(pl.multiple_of(side * (x.shape[0] // 2), 64), x.shape[0] // 2)] for x in xs]
        return [jnp.concatenate(p) if len(p) > 1 else p[0] for p in (pick(1 - model), pick(model))]
    return [x[at:at + half] for x in xs]


def load_h(h, xs, at, gain):
    half = h.shape[0] // 2
    lo, hi = x_halves(xs, at, half)
    h[:half] = normed(lo, gain[...])
    h[half:] = normed(hi, gain[...])


def rope_rows(steps, base, first, rows):
    half = rows // 2
    cos, sin = [], []
    for i in range(2):
        bc, bs = base[0, first + i:first + i + 1], base[1, first + i:first + i + 1]
        sc, ss = steps[0, :half], steps[1, :half]
        cos.append(bc * sc - bs * ss)
        sin.append(bs * sc + bc * ss)
    return jnp.concatenate(cos), jnp.concatenate(sin)


def layer_block(w, layer):
    return pl.BlockSpec((None,) + w.shape[1:], lambda *_: (layer,) + (0,) * (w.ndim - 1), pipeline_mode=pl.Buffered(1))


def rows_block(x, at, n):
    return pl.BlockSpec((pl.Element(n), pl.Element(x.shape[1])), lambda *_: (at, 0), pipeline_mode=pl.Buffered(1))


def prompt_body(at, first, *refs):
    *xs, gain, wq, wk, wv, steps, base, out, h = refs
    load_h(h, xs, at, gain)
    rows, dim = h.shape[0], wk.shape[1]
    cos, sin = rope_rows(steps, base, first, rows)
    n_q = out.shape[1] // dim - 2
    for i in range(0, n_q, 2):
        y = mm(h[...], jnp.concatenate([wq[i], wq[i + 1]], axis=1))
        out[:, i * dim:(i + 1) * dim] = rotate(y[:, :dim], cos, sin)
        out[:, (i + 1) * dim:(i + 2) * dim] = rotate(y[:, dim:], cos, sin)
    y = mm(h[...], jnp.concatenate([wk[...], wv[...]], axis=1))
    out[:, n_q * dim:(n_q + 1) * dim] = rotate(y[:, :dim], cos, sin)
    out[:, (n_q + 1) * dim:] = y[:, dim:].astype(bf16)


def prompt_qkv(xs, at, rows, gain, w, layer, steps, base, with_q, after=()):
    wq, wk, wv = w
    n_heads, d_model, dim = wq.shape[1:]
    cols = (n_heads + 2 if with_q else 2) * dim
    small = (gain, steps, base)
    return call(functools.partial(prompt_body, at, 0), 'prompt_qkv', 4 * rows * d_model * cols, 30, (1,),
                [whole(x.shape) for x in xs] + [whole(gain.shape)] + [layer_block(a, layer) for a in w] + [whole(steps.shape), whole(base.shape)],
                [jax.ShapeDtypeStruct((rows, cols), bf16)], [pltpu.VMEM((rows, d_model), bf16)],
                (*xs, gain, *w, steps, base), after)[0]


def attend(q, kbuf, vbuf, bias):
    dim, keys, masked = q.shape[1], kbuf.shape[0], bias.shape[1]
    free = keys - masked
    s = lax.dot_general(q, kbuf[...], (((1,), (1,)), ((), ())), preferred_element_type=f32)
    diag = jnp.where(bias[...] < 0, NEG_BIG, s[:, free:])
    s = jnp.concatenate([s[:, :free], diag], axis=1) if free else diag
    top = jnp.max(s, axis=-1, keepdims=True)
    e = jnp.exp2((s - top) * (LOG2E / math.sqrt(dim)))
    p = (e * (1.0 / jnp.sum(e, axis=-1, keepdims=True))).astype(bf16)
    return mm(p, vbuf[...]).astype(bf16)


def attn_body(n_x, at, first, n_kv, n_seen, prompt, *refs):
    refs = list(refs)
    take = lambda n: [refs.pop(0) for _ in range(n)]
    xs = take(n_x)
    gain, wq, wk, wv, steps, base = take(6)
    pieces, seen = take(n_kv), take(n_seen)
    qkv_p = take(1)[0] if prompt else None
    out, kv_new, h, kbuf, vbuf, bias = take(6)
    rows, dim = h.shape[0], wk.shape[1]
    half, n_q = rows // 2, wq.shape[0]
    load_h(h, xs, at, gain)
    cos, sin = rope_rows(steps, base, first, rows)
    bias[...] = causal(rows)
    fill = 0
    for r in pieces + seen:
        n = r.shape[0]
        kbuf[fill:fill + n] = r[:, :dim]
        vbuf[fill:fill + n] = r[:, dim:]
        fill += n
    y = mm(h[...], jnp.concatenate([wk[...], wv[...]], axis=1))
    k, v = rotate(y[:, :dim], cos, sin), y[:, dim:].astype(bf16)
    kv_new[:, :dim], kv_new[:, dim:] = k, v
    kbuf[fill:], vbuf[fill:] = k, v
    skip = 0
    if prompt:
        bias_p = take(1)[0]
        n_p, dev = qkv_p.shape[0], lax.axis_index('resp')
        skip = n_p // 2
        bias_p[:, :n_p] = causal(n_p)
        for s in range(1, n_kv):
            bias_p[:, s * n_p:(s + 1) * n_p] = jnp.full((n_p, n_p), jnp.where(dev >= s, 0.0, NEG_BIG), f32)
        for i in range(n_q):
            cols = slice(i * dim, (i + 1) * dim)
            mix = attend(qkv_p[:, cols], kbuf.at[:n_kv * n_p], vbuf.at[:n_kv * n_p], bias_p)
            out[:skip, cols] = mix[:skip]
            out[skip + half:2 * skip + half, cols] = mix[skip:]
    for i in range(0, n_q, 2):
        y = mm(h[...], jnp.concatenate([wq[i], wq[i + 1]], axis=1))
        for j in range(2):
            cols = slice((i + j) * dim, (i + j + 1) * dim)
            mix = attend(rotate(y[:, j * dim:(j + 1) * dim], cos, sin), kbuf, vbuf, bias)
            out[skip:skip + half, cols] = mix[:half]
            out[2 * skip + half:, cols] = mix[half:]


def attn_chunk(xs, x_specs, at, rows, gain, w, layer, steps, base, first, pieces, seen, qkv_p=None, after=()):
    wq, wk, wv = w
    n_heads, d_model, dim = wq.shape[1:]
    keys = sum(a.shape[0] for a in pieces + seen) + rows
    n_p = qkv_p.shape[0] if qkv_p is not None else 0
    extra = [qkv_p] if n_p else []
    out = [jax.ShapeDtypeStruct((rows + n_p, n_heads * dim), bf16), jax.ShapeDtypeStruct((rows, 2 * dim), bf16)]
    scratch = [pltpu.VMEM((rows, d_model), bf16), pltpu.VMEM((keys, dim), bf16), pltpu.VMEM((keys, dim), bf16), pltpu.VMEM((rows, rows), f32)]
    if n_p:
        scratch.append(pltpu.VMEM((n_p, n_p * len(pieces)), f32))
    rest = (*pieces, *seen, *extra)
    return call(functools.partial(attn_body, len(xs), at, first, len(pieces), len(seen), bool(n_p)), 'attn',
                2 * rows * d_model * n_heads * dim + 8 * rows * keys * n_heads * dim, ATTN_MIB, (1,),
                x_specs + [whole(gain.shape)] + [layer_block(a, layer) for a in w] + [whole(steps.shape), whole(base.shape)]
                + [whole(a.shape) for a in rest], out, scratch, (*xs, gain, *w, steps, base, *rest), after)


def mlp_body(n_x, at, ff, *refs):
    xs = refs[:n_x]
    a_own, a_far, wo_own, wo_far, gain, wg, wu, wd, send, keep, xm, g = refs[n_x:]
    step, blk, half = pl.program_id(0), wg.shape[1], send.shape[0]
    last = pl.num_programs(0) - 1
    rest = ff % blk or blk

    @pl.when(step == 0)
    def _():
        lo, hi = x_halves(xs, at, half)
        acc = mm(a_own[:half], wo_own[...]) + mm(a_far[half:], wo_far[...])
        g[:half] = normed((lo.astype(f32) + acc).astype(bf16), gain[...])
        acc = mm(a_own[half:], wo_own[...]) + mm(a_far[:half], wo_far[...])
        mid = (hi.astype(f32) + acc).astype(bf16)
        xm[...] = mid
        g[half:] = normed(mid, gain[...])

    def part(n):
        gate, up = mm(g[...], wg[:, :n]), mm(g[...], wu[:, :n])
        u = (gate * (1.0 / (1.0 + jnp.exp(-gate))) * up).astype(bf16)
        return mm(u, wd[:n])

    @pl.when(step == 0)
    def _():
        d = part(blk)
        send[...], keep[...] = d[:half], d[half:]

    @pl.when((step > 0) & (step < last))
    def _():
        d = part(blk)
        send[...] += d[:half]
        keep[...] += d[half:]

    @pl.when(step == last)
    def _():
        d = part(rest)
        send[...] += d[:half]
        keep[...] += d[half:]


def mlp_chunk(xs, x_specs, at, a_own, a_far, wo_own, wo_far, gain, wg, wu, wd, layer, after=()):
    rows, d_model, ff, blk = a_own.shape[0], xs[0].shape[1], wg.shape[2], FF_BLOCK
    half = rows // 2
    up_spec = pl.BlockSpec((None, d_model, blk), lambda j: (layer, 0, j))
    down_spec = pl.BlockSpec((None, blk, d_model), lambda j: (layer, j, 0))
    small = (a_own, a_far, wo_own, wo_far, gain)
    out = [jax.ShapeDtypeStruct((half, d_model), f32)] * 2 + [jax.ShapeDtypeStruct((half, d_model), bf16)]
    return call(functools.partial(mlp_body, len(xs), at, ff), 'mlp',
                6 * rows * d_model * ff + 4 * rows * d_model * wo_own.shape[0], MLP_MIB, (pl.cdiv(ff, blk),),
                x_specs + [whole(a.shape) for a in small] + [up_spec, up_spec, down_spec],
                out, [pltpu.VMEM((rows, d_model), bf16)], (*xs, *small, wg, wu, wd), after)


def head_body(row, xa, xb, gain, w, tgt, out, h, logits, top, pick):
    step, blk = pl.program_id(0), w.shape[1]

    @pl.when(step == 0)
    def _():
        load_h(h, (xa, xb), 0, gain)
        top[...] = jnp.full_like(top, NEG_BIG)
        pick[...] = jnp.zeros_like(pick)

    s = mm(h[...], w[...])
    logits[step] = s
    lanes = top.shape[1]
    hit = tgt[row:row + top.shape[0]] - step * blk
    lane = lax.broadcasted_iota(jnp.int32, top.shape, 1)
    best, found = top[...], pick[...]
    for c in range(0, blk, lanes):
        piece = s[:, c:c + lanes]
        best = jnp.maximum(best, piece)
        found += jnp.where(lane + c == hit, piece, 0.0)
    top[...], pick[...] = best, found

    @pl.when(step == pl.num_programs(0) - 1)
    def _():
        peak = jnp.max(top[...], axis=-1, keepdims=True)
        tot = jnp.zeros_like(top)
        for b in range(logits.shape[0]):
            for c in range(0, blk, lanes):
                tot += jnp.exp(logits[b, :, c:c + lanes] - peak)
        tot = jnp.sum(tot, axis=-1, keepdims=True)
        hits = jnp.sum(pick[...], axis=-1, keepdims=True)
        out[...] = jnp.where(lane == 0, peak, jnp.where(lane == 1, tot, hits))


def head_chunk(xa, xb, gain, w, tgt, row, after=()):
    d_model, vocab, blk = xa.shape[1], w.shape[1], HEAD_BLOCK
    rows = 2 * xa.shape[0]
    side = pltpu.VMEM((rows, 128), f32)
    return call(functools.partial(head_body, row), 'head', 4 * rows * d_model * vocab, HEAD_MIB, (vocab // blk,),
                [whole(xa.shape), whole(xb.shape), whole(gain.shape), pl.BlockSpec((d_model, blk), lambda j: (0, j)), whole(tgt.shape)],
                [jax.ShapeDtypeStruct((rows, 128), f32)],
                [pltpu.VMEM((rows, d_model), bf16), pltpu.VMEM((vocab // blk, rows, blk), f32), side, side],
                (xa, xb, gain, w, tgt), after)[0]


def rope_tables(positions, head_dim):
    inv_freq = jnp.exp(jnp.arange(0, head_dim, 2, dtype=f32) * (-math.log(ROPE_BASE) / head_dim))
    angles = positions.astype(f32)[:, None] * inv_freq[None, :]
    cos, sin = jnp.cos(angles), jnp.sin(angles)
    return jnp.stack([jnp.concatenate([cos, cos], axis=1), jnp.concatenate([-sin, sin], axis=1)])


def held(x, *after):
    return lax.optimization_barrier((x, *after))[0]


def solution(mesh):
    group = mesh.shape['resp']
    rows_spec = P(('prompts', 'resp'), None)
    in_specs = (rows_spec, P(('prompts', 'resp'), None, None), rows_spec, P(), P(),
                P(None, None, 'model', None), P(None, None, 'model', None), P(None, None, 'model', None),
                P(None, 'model', None, None), P(None, None, 'model'), P(None, None, 'model'),
                P(None, 'model', None), P(), P(None, 'model'))

    def across(x):
        return lax.ppermute(x, 'model', [(0, 1), (1, 0)])

    def all_pieces(x):
        return [x] + [lax.ppermute(x, 'resp', [(i, (i + s) % group) for i in range(group)]) for s in range(1, group)]

    def local_pass(x_piece, x_own, tgt_own, attn_norm, mlp_norm, w_q, w_k, w_v, w_o, w_gate, w_up, w_down, final_norm, w_head):
        n_layers, d_model, heads_loc, dim = w_q.shape
        piece_len, resp_len = x_piece.shape[0], x_own.shape[1]
        prompt_len = piece_len * group
        dev_idx, model_idx = lax.axis_index('resp'), lax.axis_index('model')
        sizes = [resp_len * n // sum(CHUNKS) for n in CHUNKS]
        starts = [sum(sizes[:c]) for c in range(len(sizes))]
        n_chunks = len(sizes)

        def sent_part(w):
            n = w.shape[0] // group
            return lax.dynamic_slice_in_dim(w, dev_idx * n, n, 0)

        def joined(part):
            return lax.all_gather(part, 'resp', axis=0, tiled=True)

        w_out = [w_o[l].reshape(heads_loc * dim, d_model) for l in range(n_layers)]
        w_heads = [[w_q[l].transpose(1, 0, 2)[None], w_k[l].reshape(1, d_model, dim), w_v[l].reshape(1, d_model, dim)]
                   for l in range(n_layers)]
        far_part = [across(sent_part(w)) for w in w_out]

        def halves(x, at, n):
            half = n // 2
            return (lax.dynamic_slice_in_dim(x, at + (1 - model_idx) * half, half, 0),
                    lax.dynamic_slice_in_dim(x, at + model_idx * half, half, 0))

        steps = rope_tables(jnp.arange(max(sizes) // 2), dim)
        both = jnp.stack([1 - model_idx, model_idx])
        base = rope_tables(jnp.concatenate([dev_idx * piece_len + both * (piece_len // 2)] + [
            prompt_len + at + both * (n // 2) for at, n in zip(starts, sizes)]), dim)
        tgt = jnp.concatenate([h for at, n in zip(starts, sizes) for h in halves(tgt_own[0] - model_idx * w_head.shape[1], at, n)])[:, None]
        x_rows = x_own[0]

        def source(l, c, with_prompt):
            n = sizes[c]
            if l == 0:
                xs = ([x_piece] if with_prompt else []) + [x_rows]
                return xs, ([whole(x_piece.shape)] if with_prompt else []) + [rows_block(x_rows, starts[c], n)], None
            return x_r[c], [whole(x.shape) for x in x_r[c]], piece_len // 2 if c == 0 else 0

        x_r = [None] * n_chunks
        pending = {}

        def mlp_of(l, c, a, wo_far, after):
            xs, specs, at = source(l, c, c == 0)
            send, keep, xm = mlp_chunk(xs, specs, at, *a, w_out[l], wo_far, mlp_norm[l][None], w_gate, w_up, w_down, l, after)
            pending[c] = (send, keep, xm)
            return keep

        def collect(c, far):
            _, keep, xm = pending.pop(c)
            mine = (xm.astype(f32) + (keep + far)).astype(bf16)
            x_r[c] = [across(mine), mine]
            return mine

        gain = attn_norm[0][None]
        qkv_p = prompt_qkv([x_piece], None, piece_len, gain, w_heads[0], 0, steps, base, True)
        pieces = all_pieces(qkv_p[:, heads_loc * dim:])
        wo_far = joined(held(far_part[0], qkv_p))
        w_heads[1] = [held(w, qkv_p) for w in w_heads[1]]
        a, seen, tail = [], [], ()
        for c in range(n_chunks):
            xs, specs, at = source(0, c, False)
            mix, kv = attn_chunk(xs, specs, at, sizes[c], gain, w_heads[0], 0, steps, base, 2 + 2 * c, pieces, list(seen),
                                 qkv_p if c == 0 else None, tail)
            seen.append(kv)
            a.append((mix, across(mix)))
            tail = (mix,)
        wo_far_next = joined(held(far_part[1], tail[0]))
        far = {}
        for c in range(n_chunks):
            tail = (mlp_of(0, c, a[c], wo_far, tail),)
            if c > 0:
                tail = (*tail, collect(c - 1, held(far[c - 1], *tail)))
            far[c] = across(held(pending[c][0], *tail))
        wo_far = wo_far_next

        gain = attn_norm[1][None]
        pieces = all_pieces(prompt_qkv(x_r[0], 0, piece_len, gain, w_heads[1], 0, steps, base, False, tail))
        a, seen = [], []
        done = 0
        for c in range(n_chunks):
            if c == n_chunks - 1:
                tail = (*tail, collect(c, far[c]))
            xs, specs, at = source(1, c, False)
            mix, kv = attn_chunk(xs, specs, at, sizes[c], gain, w_heads[1], 0, steps, base, 2 + 2 * c, pieces, list(seen), None, tail)
            seen.append(kv)
            a.append((mix, across(mix)))
            tail = (mix,)
            if c == n_chunks - 2:
                tail = (mlp_of(1, done, a[done], wo_far, tail),)
                far[done] = across(pending[done][0])
                done += 1
        while done < n_chunks:
            tail = (mlp_of(1, done, a[done], wo_far, tail),)
            tail = (*tail, collect(done - 1, held(far[done - 1], *tail)))
            far[done] = across(held(pending[done][0], *tail))
            done += 1
        stats = []
        for c in range(n_chunks):
            if c == n_chunks - 1:
                collect(c, held(far[c], *tail))
            stats.append(head_chunk(*x_r[c], final_norm[None], w_head, tgt, starts[c], tail))
            tail = (stats[-1],)
        here = jnp.concatenate([h for s, n in zip(stats, sizes) for h in halves(s[:, :3], 0, n)]).T
        there = across(here)
        top = jnp.maximum(here[0], there[0])
        tot = here[1] * jnp.exp(here[0] - top) + there[1] * jnp.exp(there[0] - top)
        logp = here[2] + there[2] - top - jnp.log(tot)
        return logp[None, :]

    return jax.shard_map(local_pass, mesh=mesh, in_specs=in_specs, out_specs=rows_spec, check_vma=False)
```

time: 1010 us -> 399 us (0.40)
  waiting for transfers between devices: 615 us -> 57.3 us
  matrix products: 250 us -> 0 us
  Pallas kernels: 0 us -> 248 us
  other arithmetic: 76.9 us -> 8.77 us
  starting transfers between devices: 0.98 us -> 32.4 us
  blocking collectives: 29.9 us -> 0 us
  local copies, waits for them, and re-layouts: 23 us -> 34.4 us
    psum x4 -> x0, waiting for transfers between devices: 615 us -> none  [the longest x2 310 us: finish_layer(): lax.psum(jnp.einsum('the,hed->td', attn_mix, w_out, preferred_element_typ...]
    pallas_call x0 -> x17, Pallas kernels: none -> 248 us  [call(): pl.pallas_call(run, name=name, grid=grid, in_specs=list(in_specs) + [ORDE...]
    dot_general x15 -> x0, matrix products: 243 us -> none  [the longest x2 48.1 us: finish_layer(): up_proj = jnp.dot(hidden, w_up_l, preferred_element_type=jnp.float32)]
    reduce_sum x8 -> x0, other arithmetic: 60.9 us -> none  [the longest x2 33.6 us: attend_local(): attn_probs = jax.nn.softmax(scores, axis=-1).astype(jnp.bfloat16)]
    ppermute x0 -> x27, waiting for transfers between devices: none -> 57.2 us  [the longest x21 57.2 us: across(): return lax.ppermute(x, 'model', [(0, 1), (1, 0)])]
    ppermute x0 -> x27, starting transfers between devices: none -> 32.2 us  [the longest x21 25.5 us: across(): return lax.ppermute(x, 'model', [(0, 1), (1, 0)])]
    all_gather x2 -> x0, blocking collectives: 19.9 us -> none  [local_pass(): lax.all_gather(jnp.stack([k_tok[:piece_len], v_tok[:piece_len]]), 'resp',...]
  transfers between devices with their start and end apart: 4 -> 29, of which waited for: 4 -> 8; matrix products, arithmetic and copies ran while one was open for 1% -> 6% of each run, Pallas kernels for 0% -> 60%
where the time goes in v1:
time: 399 us; the launch traced here: 395 us
  Pallas kernels  248 us (62%)
  waiting for transfers between devices  57.3 us (14%)
  local copies, waits for them, and re-layouts  34.4 us (9%)
  starting transfers between devices  32.4 us (8%)
  between operations  14.2 us (4%)
  other arithmetic  8.77 us (2%)
    pallas_call x17, Pallas kernels, call(): pl.pallas_call(run, name=name, grid=grid, in_specs=list(in_specs) + [ORDE...  248 us
    ppermute x21, waiting for transfers between devices, across(): return lax.ppermute(x, 'model', [(0, 1), (1, 0)])  57.2 us
    ppermute x21, starting transfers between devices, across(): return lax.ppermute(x, 'model', [(0, 1), (1, 0)])  25.5 us
    unnamed x98, local copies, waits for them, and re-layouts  13.7 us
  transfers between devices with their start and end apart: 29, of which 8 were waited for; matrix products, arithmetic and copies ran while one was open for 6% of the time, Pallas kernels for 60%

profile of v1, /device:TPU:0, one launch (start us, length us, event | category | flops | bytes accessed | tf_op | source)
XLA Modules:
  0.0 395.1 jit_solution(3962426593986820818)
XLA Ops:
  6.5 4.2 %fusion.8 = (bf16[1,6,128,1536]{3,2,1,0:T(8,128)(2,1)}, bf16[1,6,128,1536]{3,2,1,0:T(8,128)(2,1)S(1)}) fusion(bf16[2,6,128,1536]{3,2,1,0:T(8,128)(2,1)} %param.22), kind=kLoop, calls=%fused_computation.57 | loop fusion | bytes 9437184 | tf_op jit(solution)/shard_map/slice | solution.py:340
  11.6 3.4 collective-permute-start.4
  15.8 4.2 %slice_bitcast_fusion = (bf16[1,6,1536,128]{3,2,1,0:T(8,128)(2,1)}, bf16[1,6,1536,128]{3,2,1,0:T(8,128)(2,1)S(1)}) fusion(bf16[2,1536,6,128]{3,1,2,0:T(8,128)(2,1)} %param.19), kind=kLoop, calls=%fused_computation | loop fusion | bytes 9437184 | tf_op jit(solution)/shard_map/broadcast_in_dim | solution.py:341
  24.4 3.9 collective-permute-done.4
  29.5 1.7 collective-permute-start.1
  36.1 1.7 copy-done.2
  37.7 8.4 %attn.6 = (bf16[384,768]{1,0:T(8,128)(2,1)}, bf16[256,256]{1,0:T(8,128)(2,1)S(1)}) custom-call(bf16[1024,1536]{1,0:T(8,128)(2,1)S(1)} %bitcast.49, f32[1,1536]{1,0:T(1,128)S(1)} %get-tuple-element.110.refs_1_, bf16[1,6,1536,128]{3,2,1,0:T(8,128)(2,1)S(1)} %copy-done.2, bf16[1,1536,128]{2,1,0:T(8,128)(2,1)S(1)} %copy-done.8, ...), custom_call_target="tpu_custom_call" | custom-call | flops 1811939328 | tf_op jit(solution)/shard_map/attn/pallas_call | solution.py:44
  46.6 9.4 %attn.7 = (bf16[384,768]{1,0:T(8,128)(2,1)}, bf16[384,256]{1,0:T(8,128)(2,1)S(1)}) custom-call(bf16[1024,1536]{1,0:T(8,128)(2,1)S(1)} %bitcast.50, f32[1,1536]{1,0:T(1,128)S(1)} %get-tuple-element.110.refs_1_, bf16[1,6,1536,128]{3,2,1,0:T(8,128)(2,1)S(1)} %copy-done.2, bf16[1,1536,128]{2,1,0:T(8,128)(2,1)S(1)} %copy-done.8, ...), custom_call_target="tpu_custom_call" | custom-call | flops 3623878656 | tf_op jit(solution)/shard_map/attn/pallas_call | solution.py:44
  57.5 9.2 %attn.8 = (bf16[384,768]{1,0:T(8,128)(2,1)}, bf16[384,256]{1,0:T(8,128)(2,1)}) custom-call(bf16[1024,1536]{1,0:T(8,128)(2,1)S(1)} %bitcast.51, f32[1,1536]{1,0:T(1,128)S(1)} %get-tuple-element.110.refs_1_, bf16[1,6,1536,128]{3,2,1,0:T(8,128)(2,1)S(1)} %copy-done.2, bf16[1,1536,128]{2,1,0:T(8,128)(2,1)S(1)} %copy-done.8, ...), custom_call_target="tpu_custom_call" | custom-call | flops 4529848320 | tf_op jit(solution)/shard_map/attn/pallas_call | solution.py:44
  67.2 27.3 %mlp.6 = (f32[192,1536]{1,0:T(8,128)}, f32[192,1536]{1,0:T(8,128)}, bf16[192,1536]{1,0:T(8,128)(2,1)}) custom-call(bf16[128,1536]{1,0:T(8,128)(2,1)} %refs_0_.3, bf16[1024,1536]{1,0:T(8,128)(2,1)} %bitcast.46, bf16[384,768]{1,0:T(8,128)(2,1)} %get-tuple-element.48.refs_12_.refs_2_, bf16[384,768]{1,0:T(8,128)(2,1)} %collective-permute-done.3.refs_3_, ...), custom_call_target="tpu_custom_call" | custom-call | flops 17666408448 | tf_op jit(solution)/shard_map/mlp/pallas_call | solution.py:44
  96.1 27.0 %mlp.7 = (f32[192,1536]{1,0:T(8,128)}, f32[192,1536]{1,0:T(8,128)}, bf16[192,1536]{1,0:T(8,128)(2,1)}) custom-call(bf16[1024,1536]{1,0:T(8,128)(2,1)} %bitcast.47, bf16[384,768]{1,0:T(8,128)(2,1)} %get-tuple-element.52.refs_13_.refs_1_, bf16[384,768]{1,0:T(8,128)(2,1)} %collective-permute-done.6.refs_2_, bf16[768,1536]{1,0:T(8,128)(2,1)} %bitcast.58, ...), custom_call_target="tpu_custom_call" | custom-call | flops 17666408448 | tf_op jit(solution)/shard_map/mlp/pallas_call | solution.py:44
  127.1 27.3 %mlp.8 = (f32[192,1536]{1,0:T(8,128)}, f32[192,1536]{1,0:T(8,128)}, bf16[192,1536]{1,0:T(8,128)(2,1)}) custom-call(bf16[1024,1536]{1,0:T(8,128)(2,1)} %bitcast.48, bf16[384,768]{1,0:T(8,128)(2,1)} %get-tuple-element.53.refs_10_.refs_1_, bf16[384,768]{1,0:T(8,128)(2,1)} %copy-done.42, bf16[768,1536]{1,0:T(8,128)(2,1)} %bitcast.59, ...), custom_call_target="tpu_custom_call" | custom-call | flops 17666408448 | tf_op jit(solution)/shard_map/mlp/pallas_call | solution.py:44
  154.4 8.5 %collective-permute-done.9 = f32[192,1536]{1,0:T(8,128)S(1)} collective-permute-done((f32[192,1536]{1,0:T(8,128)}, f32[192,1536]{1,0:T(8,128)S(1)}, u32[]{:S(2)}, u32[]{:S(2)}) %collective-permute-start.9) | collective-permute-done | bytes 1179680 | tf_op jit(solution)/shard_map/ppermute | solution.py:319
  164.0 2.2 add_convert_fusion.3.refs_9_.refs_13_.refs_1_
  171.9 2.3 prompt_qkv.3.refs_8_
  174.2 2.1 collective-permute-start.11
  179.7 1.7 copy.20.refs_4_
  185.0 7.5 %attn.9 = (bf16[256,768]{1,0:T(8,128)(2,1)}, bf16[256,256]{1,0:T(8,128)(2,1)S(1)}) custom-call(bf16[192,1536]{1,0:T(8,128)(2,1)} %collective-permute-done.7.refs_0_, bf16[192,1536]{1,0:T(8,128)(2,1)} %add_convert_fusion.4.refs_10_.refs_1_, f32[1,1536]{1,0:T(1,128)S(1)} %copy-done.22, bf16[1,6,1536,128]{3,2,1,0:T(8,128)(2,1)S(1)} %copy-done.3, ...), custom_call_target="tpu_custom_call" | custom-call | flops 1811939328 | tf_op jit(solution)/shard_map/attn/pallas_call | solution.py:44
  193.4 14.3 %collective-permute-done.15.refs_0_ = bf16[192,1536]{1,0:T(8,128)(2,1)} collective-permute-done((bf16[192,1536]{1,0:T(8,128)(2,1)S(1)}, bf16[192,1536]{1,0:T(8,128)(2,1)}, u32[]{:S(2)}, u32[]{:S(2)}) %collective-permute-start.15) | collective-permute-done | bytes 589856 | tf_op jit(solution)/shard_map/ppermute | solution.py:319
  207.7 10.9 %attn.10 = (bf16[384,768]{1,0:T(8,128)(2,1)}, bf16[384,256]{1,0:T(8,128)(2,1)S(1)}) custom-call(bf16[192,1536]{1,0:T(8,128)(2,1)} %collective-permute-done.15.refs_0_, bf16[192,1536]{1,0:T(8,128)(2,1)S(1)} %add_convert_fusion.3.refs_9_.refs_13_.refs_1_, f32[1,1536]{1,0:T(1,128)S(1)} %copy-done.22, bf16[1,6,1536,128]{3,2,1,0:T(8,128)(2,1)S(1)} %copy-done.3, ...), custom_call_target="tpu_custom_call" | custom-call | flops 3623878656 | tf_op jit(solution)/shard_map/attn/pallas_call | solution.py:44
  222.2 22.5 %mlp.9 = (f32[128,1536]{1,0:T(8,128)}, f32[128,1536]{1,0:T(8,128)}, bf16[128,1536]{1,0:T(8,128)(2,1)}) custom-call(bf16[192,1536]{1,0:T(8,128)(2,1)} %collective-permute-done.7.refs_0_, bf16[192,1536]{1,0:T(8,128)(2,1)} %add_convert_fusion.4.refs_10_.refs_1_, bf16[256,768]{1,0:T(8,128)(2,1)} %get-tuple-element.68.refs_13_.refs_2_, ...), custom_call_target="tpu_custom_call" | custom-call | flops 11777605632 | tf_op jit(solution)/shard_map/mlp/pallas_call | solution.py:44
  248.3 10.4 %attn.11 = (bf16[384,768]{1,0:T(8,128)(2,1)}, bf16[384,256]{1,0:T(8,128)(2,1)}) custom-call(bf16[192,1536]{1,0:T(8,128)(2,1)} %collective-permute-done.19.refs_0_, bf16[192,1536]{1,0:T(8,128)(2,1)S(1)} %add_convert_fusion.2.refs_1_.refs_15_, f32[1,1536]{1,0:T(1,128)S(1)} %copy-done.22, bf16[1,6,1536,128]{3,2,1,0:T(8,128)(2,1)S(1)} %copy-done.3, ...), custom_call_target="tpu_custom_call" | custom-call | flops 4529848320 | tf_op jit(solution)/shard_map/attn/pallas_call | solution.py:44
  259.2 27.1 %mlp.10 = (f32[192,1536]{1,0:T(8,128)}, f32[192,1536]{1,0:T(8,128)}, bf16[192,1536]{1,0:T(8,128)(2,1)}) custom-call(bf16[192,1536]{1,0:T(8,128)(2,1)} %collective-permute-done.15.refs_0_, bf16[192,1536]{1,0:T(8,128)(2,1)} %copy-done.4, bf16[384,768]{1,0:T(8,128)(2,1)} %get-tuple-element.71.refs_10_.refs_2_, ...), custom_call_target="tpu_custom_call" | custom-call | flops 17666408448 | tf_op jit(solution)/shard_map/mlp/pallas_call | solution.py:44
  290.5 27.2 %mlp.11 = (f32[192,1536]{1,0:T(8,128)}, f32[192,1536]{1,0:T(8,128)}, bf16[192,1536]{1,0:T(8,128)(2,1)}) custom-call(bf16[192,1536]{1,0:T(8,128)(2,1)} %collective-permute-done.19.refs_0_, bf16[192,1536]{1,0:T(8,128)(2,1)} %copy-done.12, bf16[384,768]{1,0:T(8,128)(2,1)} %get-tuple-element.79.refs_10_.refs_2_, bf16[384,768]{1,0:T(8,128)(2,1)} %copy-done.35, ...), custom_call_target="tpu_custom_call" | custom-call | flops 17666408448 | tf_op jit(solution)/shard_map/mlp/pallas_call | solution.py:44
  317.6 4.2 %collective-permute-done.22 = f32[192,1536]{1,0:T(8,128)S(1)} collective-permute-done((f32[192,1536]{1,0:T(8,128)}, f32[192,1536]{1,0:T(8,128)S(1)}, u32[]{:S(2)}, u32[]{:S(2)}) %collective-permute-start.22) | collective-permute-done | bytes 1179680 | tf_op jit(solution)/shard_map/ppermute | solution.py:319
  324.1 9.1 %head.3.refs_5_ = f32[256,128]{1,0:T(8,128)} custom-call(bf16[128,1536]{1,0:T(8,128)(2,1)} %collective-permute-done.20.refs_0_, bf16[128,1536]{1,0:T(8,128)(2,1)} %copy-done.30, f32[1,1536]{1,0:T(1,128)} %broadcast_in_dim.10.refs_2_, bf16[1536,4096]{1,0:T(8,128)(2,1)} %refs_3_.5, s32[1024,1]{1,0:T(8,128)} %copy.20.refs_4_, ...), custom_call_target="tpu_custom_call" | custom-call | flops 6442450944 | tf_op jit(solution)/shard_map/head/pallas_call | solution.py:44
  333.2 5.1 %collective-permute-done.23.refs_0_ = bf16[192,1536]{1,0:T(8,128)(2,1)} collective-permute-done((bf16[192,1536]{1,0:T(8,128)(2,1)S(1)}, bf16[192,1536]{1,0:T(8,128)(2,1)}, u32[]{:S(2)}, u32[]{:S(2)}) %collective-permute-start.23) | collective-permute-done | bytes 589856 | tf_op jit(solution)/shard_map/ppermute | solution.py:319
  338.3 11.1 %head.4.refs_5_ = f32[384,128]{1,0:T(8,128)} custom-call(bf16[192,1536]{1,0:T(8,128)(2,1)} %collective-permute-done.23.refs_0_, bf16[192,1536]{1,0:T(8,128)(2,1)} %copy-done.41, f32[1,1536]{1,0:T(1,128)} %broadcast_in_dim.10.refs_2_, bf16[1536,4096]{1,0:T(8,128)(2,1)} %refs_3_.5, s32[1024,1]{1,0:T(8,128)} %copy.20.refs_4_, f32[256,128]{1,0:T(8,128)} %head.3.refs_5_), custom_call_target="tpu_custom_call" | custom-call | flops 9663676416 | tf_op jit(solution)/shard_map/head/pallas_call | solution.py:44
  349.4 11.2 %collective-permute-done.24 = f32[192,1536]{1,0:T(8,128)S(1)} collective-permute-done((f32[192,1536]{1,0:T(8,128)}, f32[192,1536]{1,0:T(8,128)S(1)}, u32[]{:S(2)}, u32[]{:S(2)}) %collective-permute-start.24) | collective-permute-done | bytes 1179680 | tf_op jit(solution)/shard_map/ppermute | solution.py:319
  362.8 7.9 %collective-permute-done.25.refs_0_ = bf16[192,1536]{1,0:T(8,128)(2,1)S(1)} collective-permute-done((bf16[192,1536]{1,0:T(8,128)(2,1)S(1)}, bf16[192,1536]{1,0:T(8,128)(2,1)S(1)}, u32[]{:S(2)}, u32[]{:S(2)}) %collective-permute-start.25) | collective-permute-done | bytes 589856 | tf_op jit(solution)/shard_map/ppermute | solution.py:319
  371.6 10.8 %head.5 = f32[384,128]{1,0:T(8,128)} custom-call(bf16[192,1536]{1,0:T(8,128)(2,1)} %copy-done.48, bf16[192,1536]{1,0:T(8,128)(2,1)} %copy-done.37, f32[1,1536]{1,0:T(1,128)} %broadcast_in_dim.10.refs_2_, bf16[1536,4096]{1,0:T(8,128)(2,1)} %refs_3_.5, s32[1024,1]{1,0:T(8,128)} %copy.20.refs_4_, f32[384,128]{1,0:T(8,128)} %head.4.refs_5_), custom_call_target="tpu_custom_call" | custom-call | flops 9663676416 | tf_op jit(solution)/shard_map/head/pallas_call | solution.py:44
  385.2 2.1 collective-permute-done.26
  (185 shorter events, 55.3 us)
Async XLA Ops:
  6.5 60.7 %all-gather.3.cloned.1.call-start = ((), (), s32[]{:S(2)}) async-start(), calls=%async_computation | async-start | bytes 2949120 | tf_op jit(solution)/shard_map/all_gather | solution.py:338
  11.6 16.7 %collective-permute-start.4 = (bf16[192,1536]{1,0:T(8,128)(2,1)}, bf16[192,1536]{1,0:T(8,128)(2,1)}, u32[]{:S(2)}, u32[]{:S(2)}) collective-permute-start(bf16[192,1536]{1,0:T(8,128)(2,1)} %constant_dynamic-slice_fusion.13), channel_id=1, source_target_pairs={{0,4},{4,0},{1,5},{5,1},{2,6},{6,2},{3,7},{7,3}} | collective-permute-start | bytes 1769480 | tf_op jit(solution)/shard_map/ppermute | solution.py:319
  28.4 193.8 %all-gather.5.cloned.1.call-start = ((), (), s32[]{:S(2)}) async-start(), calls=%async_computation.1 | async-start | bytes 2949120 | tf_op jit(solution)/shard_map/all_gather | solution.py:338
  29.5 6.5 %collective-permute-start = (bf16[128,256]{1,0:T(8,128)(2,1)S(1)}, bf16[128,256]{1,0:T(8,128)(2,1)S(1)}, u32[]{:S(2)}, u32[]{:S(2)}) collective-permute-start(bf16[128,256]{1,0:T(8,128)(2,1)S(1)} %slice.94.refs_7_), channel_id=1, source_target_pairs={{0,1},{1,2},{2,3},{3,0},{4,5},{5,6},{6,7},{7,4}} | collective-permute-start | bytes 196616 | tf_op jit(solution)/shard_map/ppermute | solution.py:322
  29.5 6.5 %collective-permute-start.1 = (bf16[128,256]{1,0:T(8,128)(2,1)S(1)}, bf16[128,256]{1,0:T(8,128)(2,1)S(1)}, u32[]{:S(2)}, u32[]{:S(2)}) collective-permute-start(bf16[128,256]{1,0:T(8,128)(2,1)S(1)} %slice.94.refs_7_), channel_id=1, source_target_pairs={{0,2},{1,3},{2,0},{3,1},{4,6},{5,7},{6,4},{7,5}} | collective-permute-start | bytes 196616 | tf_op jit(solution)/shard_map/ppermute | solution.py:322
  31.3 4.7 %collective-permute-start.2 = (bf16[128,256]{1,0:T(8,128)(2,1)S(1)}, bf16[128,256]{1,0:T(8,128)(2,1)S(1)}, u32[]{:S(2)}, u32[]{:S(2)}) collective-permute-start(bf16[128,256]{1,0:T(8,128)(2,1)S(1)} %slice.94.refs_7_), channel_id=1, source_target_pairs={{0,3},{1,0},{2,1},{3,2},{4,7},{5,4},{6,5},{7,6}} | collective-permute-start | bytes 196616 | tf_op jit(solution)/shard_map/ppermute | solution.py:322
  33.8 33.3 %collective-permute-start.14 = (bf16[192,1536]{1,0:T(8,128)(2,1)S(1)}, bf16[192,1536]{1,0:T(8,128)(2,1)}, u32[]{:S(2)}, u32[]{:S(2)}) collective-permute-start(bf16[192,1536]{1,0:T(8,128)(2,1)S(1)} %constant_dynamic-slice_fusion.12), channel_id=1, source_target_pairs={{0,4},{4,0},{1,5},{5,1},{2,6},{6,2},{3,7},{7,3}} | collective-permute-start | bytes 1769480 | tf_op jit(solution)/shard_map/ppermute | solution.py:319
  46.1 21.1 %collective-permute-start.3 = (bf16[384,768]{1,0:T(8,128)(2,1)}, bf16[384,768]{1,0:T(8,128)(2,1)}, u32[]{:S(2)}, u32[]{:S(2)}) collective-permute-start(bf16[384,768]{1,0:T(8,128)(2,1)} %get-tuple-element.48.refs_12_.refs_2_), channel_id=1, source_target_pairs={{0,4},{4,0},{1,5},{5,1},{2,6},{6,2},{3,7},{7,3}} | collective-permute-start | bytes 1769480 | tf_op jit(solution)/shard_map/ppermute | solution.py:319
  56.0 40.1 %collective-permute-start.6 = (bf16[384,768]{1,0:T(8,128)(2,1)}, bf16[384,768]{1,0:T(8,128)(2,1)}, u32[]{:S(2)}, u32[]{:S(2)}) collective-permute-start(bf16[384,768]{1,0:T(8,128)(2,1)} %get-tuple-element.52.refs_13_.refs_1_), channel_id=1, source_target_pairs={{0,4},{4,0},{1,5},{5,1},{2,6},{6,2},{3,7},{7,3}} | collective-permute-start | bytes 1769480 | tf_op jit(solution)/shard_map/ppermute | solution.py:319
  66.6 59.6 %collective-permute-start.8 = (bf16[384,768]{1,0:T(8,128)(2,1)}, bf16[384,768]{1,0:T(8,128)(2,1)S(1)}, u32[]{:S(2)}, u32[]{:S(2)}) collective-permute-start(bf16[384,768]{1,0:T(8,128)(2,1)} %get-tuple-element.53.refs_10_.refs_1_), channel_id=1, source_target_pairs={{0,4},{4,0},{1,5},{5,1},{2,6},{6,2},{3,7},{7,3}} | collective-permute-start | bytes 1769480 | tf_op jit(solution)/shard_map/ppermute | solution.py:319
  94.5 28.6 %collective-permute-start.5 = (f32[192,1536]{1,0:T(8,128)}, f32[192,1536]{1,0:T(8,128)S(1)}, u32[]{:S(2)}, u32[]{:S(2)}) collective-permute-start(f32[192,1536]{1,0:T(8,128)} %get-tuple-element.57), channel_id=1, source_target_pairs={{0,4},{4,0},{1,5},{5,1},{2,6},{6,2},{3,7},{7,3}} | collective-permute-start | bytes 3538952 | tf_op jit(solution)/shard_map/ppermute | solution.py:319
  124.2 45.4 %collective-permute-start.7 = (bf16[192,1536]{1,0:T(8,128)(2,1)}, bf16[192,1536]{1,0:T(8,128)(2,1)}, u32[]{:S(2)}, u32[]{:S(2)}) collective-permute-start(bf16[192,1536]{1,0:T(8,128)(2,1)} %add_convert_fusion.4.refs_10_.refs_1_), channel_id=1, source_target_pairs={{0,4},{4,0},{1,5},{5,1},{2,6},{6,2},{3,7},{7,3}} | collective-permute-start | bytes 1769480 | tf_op jit(solution)/shard_map/ppermute | solution.py:319
  124.7 38.2 %collective-permute-start.9 = (f32[192,1536]{1,0:T(8,128)}, f32[192,1536]{1,0:T(8,128)S(1)}, u32[]{:S(2)}, u32[]{:S(2)}) collective-permute-start(f32[192,1536]{1,0:T(8,128)} %get-tuple-element.66), channel_id=1, source_target_pairs={{0,4},{4,0},{1,5},{5,1},{2,6},{6,2},{3,7},{7,3}} | collective-permute-start | bytes 3538952 | tf_op jit(solution)/shard_map/ppermute | solution.py:319
  166.2 41.5 %copy-start.4 = (bf16[192,1536]{1,0:T(8,128)(2,1)}, bf16[192,1536]{1,0:T(8,128)(2,1)S(1)}, u32[]{:S(2)}) copy-start(bf16[192,1536]{1,0:T(8,128)(2,1)S(1)} %add_convert_fusion.3.refs_9_.refs_13_.refs_1_) | copy-start | bytes 1769476
  166.2 54.0 %collective-permute-start.18 = (f32[192,1536]{1,0:T(8,128)}, f32[192,1536]{1,0:T(8,128)}, u32[]{:S(2)}, u32[]{:S(2)}) collective-permute-start(f32[192,1536]{1,0:T(8,128)} %get-tuple-element.77), channel_id=1, source_target_pairs={{0,4},{4,0},{1,5},{5,1},{2,6},{6,2},{3,7},{7,3}} | collective-permute-start | bytes 3538952 | tf_op jit(solution)/shard_map/ppermute | solution.py:319
  167.8 39.9 %collective-permute-start.15 = (bf16[192,1536]{1,0:T(8,128)(2,1)S(1)}, bf16[192,1536]{1,0:T(8,128)(2,1)}, u32[]{:S(2)}, u32[]{:S(2)}) collective-permute-start(bf16[192,1536]{1,0:T(8,128)(2,1)S(1)} %add_convert_fusion.3.refs_9_.refs_13_.refs_1_), channel_id=1, source_target_pairs={{0,4},{4,0},{1,5},{5,1},{2,6},{6,2},{3,7},{7,3}} | collective-permute-start | bytes 1769480 | tf_op jit(solution)/shard_map/ppermute | solution.py:319
  174.2 8.5 %collective-permute-start.10 = (bf16[128,256]{1,0:T(8,128)(2,1)}, bf16[128,256]{1,0:T(8,128)(2,1)}, u32[]{:S(2)}, u32[]{:S(2)}) collective-permute-start(bf16[128,256]{1,0:T(8,128)(2,1)} %prompt_qkv.3.refs_8_), channel_id=1, source_target_pairs={{0,1},{1,2},{2,3},{3,0},{4,5},{5,6},{6,7},{7,4}} | collective-permute-start | bytes 196616 | tf_op jit(solution)/shard_map/ppermute | solution.py:322
  174.2 8.5 %collective-permute-start.11 = (bf16[128,256]{1,0:T(8,128)(2,1)}, bf16[128,256]{1,0:T(8,128)(2,1)}, u32[]{:S(2)}, u32[]{:S(2)}) collective-permute-start(bf16[128,256]{1,0:T(8,128)(2,1)} %prompt_qkv.3.refs_8_), channel_id=1, source_target_pairs={{0,2},{1,3},{2,0},{3,1},{4,6},{5,7},{6,4},{7,5}} | collective-permute-start | bytes 196616 | tf_op jit(solution)/shard_map/ppermute | solution.py:322
  176.3 6.4 %collective-permute-start.12 = (bf16[128,256]{1,0:T(8,128)(2,1)}, bf16[128,256]{1,0:T(8,128)(2,1)}, u32[]{:S(2)}, u32[]{:S(2)}) collective-permute-start(bf16[128,256]{1,0:T(8,128)(2,1)} %prompt_qkv.3.refs_8_), channel_id=1, source_target_pairs={{0,3},{1,0},{2,1},{3,2},{4,7},{5,4},{6,5},{7,6}} | collective-permute-start | bytes 196616 | tf_op jit(solution)/shard_map/ppermute | solution.py:322
  192.5 29.7 %collective-permute-start.13 = (bf16[256,768]{1,0:T(8,128)(2,1)}, bf16[256,768]{1,0:T(8,128)(2,1)}, u32[]{:S(2)}, u32[]{:S(2)}) collective-permute-start(bf16[256,768]{1,0:T(8,128)(2,1)} %get-tuple-element.68.refs_13_.refs_2_), channel_id=1, source_target_pairs={{0,4},{4,0},{1,5},{5,1},{2,6},{6,2},{3,7},{7,3}} | collective-permute-start | bytes 1179656 | tf_op jit(solution)/shard_map/ppermute | solution.py:319
  218.6 40.7 %collective-permute-start.17 = (bf16[384,768]{1,0:T(8,128)(2,1)}, bf16[384,768]{1,0:T(8,128)(2,1)}, u32[]{:S(2)}, u32[]{:S(2)}) collective-permute-start(bf16[384,768]{1,0:T(8,128)(2,1)} %get-tuple-element.71.refs_10_.refs_2_), channel_id=1, source_target_pairs={{0,4},{4,0},{1,5},{5,1},{2,6},{6,2},{3,7},{7,3}} | collective-permute-start | bytes 1769480 | tf_op jit(solution)/shard_map/ppermute | solution.py:319
  221.7 24.6 %collective-permute-start.19 = (bf16[192,1536]{1,0:T(8,128)(2,1)S(1)}, bf16[192,1536]{1,0:T(8,128)(2,1)}, u32[]{:S(2)}, u32[]{:S(2)}) collective-permute-start(bf16[192,1536]{1,0:T(8,128)(2,1)S(1)} %add_convert_fusion.2.refs_1_.refs_15_), channel_id=1, source_target_pairs={{0,4},{4,0},{1,5},{5,1},{2,6},{6,2},{3,7},{7,3}} | collective-permute-start | bytes 1769480 | tf_op jit(solution)/shard_map/ppermute | solution.py:319
  244.7 41.6 %collective-permute-start.16 = (f32[128,1536]{1,0:T(8,128)}, f32[128,1536]{1,0:T(8,128)}, u32[]{:S(2)}, u32[]{:S(2)}) collective-permute-start(f32[128,1536]{1,0:T(8,128)} %get-tuple-element.74), channel_id=1, source_target_pairs={{0,4},{4,0},{1,5},{5,1},{2,6},{6,2},{3,7},{7,3}} | collective-permute-start | bytes 2359304 | tf_op jit(solution)/shard_map/ppermute | solution.py:319
  258.8 30.9 %collective-permute-start.21 = (bf16[384,768]{1,0:T(8,128)(2,1)}, bf16[384,768]{1,0:T(8,128)(2,1)S(1)}, u32[]{:S(2)}, u32[]{:S(2)}) collective-permute-start(bf16[384,768]{1,0:T(8,128)(2,1)} %get-tuple-element.79.refs_10_.refs_2_), channel_id=1, source_target_pairs={{0,4},{4,0},{1,5},{5,1},{2,6},{6,2},{3,7},{7,3}} | collective-permute-start | bytes 1769480 | tf_op jit(solution)/shard_map/ppermute | solution.py:319
  287.6 36.5 %collective-permute-start.20 = (bf16[128,1536]{1,0:T(8,128)(2,1)S(1)}, bf16[128,1536]{1,0:T(8,128)(2,1)}, u32[]{:S(2)}, u32[]{:S(2)}) collective-permute-start(bf16[128,1536]{1,0:T(8,128)(2,1)S(1)} %add_convert_fusion.5.refs_11_.refs_1_), channel_id=1, source_target_pairs={{0,4},{4,0},{1,5},{5,1},{2,6},{6,2},{3,7},{7,3}} | collective-permute-start | bytes 1179656 | tf_op jit(solution)/shard_map/ppermute | solution.py:319
  289.2 32.6 %copy-start.28 = (f32[192,1536]{1,0:T(8,128)S(1)}, f32[192,1536]{1,0:T(8,128)}, u32[]{:S(2)}) copy-start(f32[192,1536]{1,0:T(8,128)} %get-tuple-element.80.refs_10_) | copy-start | bytes 3538948
  289.2 32.6 %copy-start.39 = (bf16[192,1536]{1,0:T(8,128)(2,1)S(1)}, bf16[192,1536]{1,0:T(8,128)(2,1)}, u32[]{:S(2)}) copy-start(bf16[192,1536]{1,0:T(8,128)(2,1)} %get-tuple-element.83) | copy-start | bytes 1769476
  289.2 32.6 %collective-permute-start.22 = (f32[192,1536]{1,0:T(8,128)}, f32[192,1536]{1,0:T(8,128)S(1)}, u32[]{:S(2)}, u32[]{:S(2)}) collective-permute-start(f32[192,1536]{1,0:T(8,128)} %get-tuple-element.85), channel_id=1, source_target_pairs={{0,4},{4,0},{1,5},{5,1},{2,6},{6,2},{3,7},{7,3}} | collective-permute-start | bytes 3538952 | tf_op jit(solution)/shard_map/ppermute | solution.py:319
  322.1 16.2 %collective-permute-start.23 = (bf16[192,1536]{1,0:T(8,128)(2,1)S(1)}, bf16[192,1536]{1,0:T(8,128)(2,1)}, u32[]{:S(2)}, u32[]{:S(2)}) collective-permute-start(bf16[192,1536]{1,0:T(8,128)(2,1)S(1)} %add_convert_fusion.1.refs_6_.refs_1_), channel_id=1, source_target_pairs={{0,4},{4,0},{1,5},{5,1},{2,6},{6,2},{3,7},{7,3}} | collective-permute-start | bytes 1769480 | tf_op jit(solution)/shard_map/ppermute | solution.py:319
  323.7 36.9 %collective-permute-start.24 = (f32[192,1536]{1,0:T(8,128)}, f32[192,1536]{1,0:T(8,128)S(1)}, u32[]{:S(2)}, u32[]{:S(2)}) collective-permute-start(f32[192,1536]{1,0:T(8,128)} %get-tuple-element.89), channel_id=1, source_target_pairs={{0,4},{4,0},{1,5},{5,1},{2,6},{6,2},{3,7},{7,3}} | collective-permute-start | bytes 3538952 | tf_op jit(solution)/shard_map/ppermute | solution.py:319
  360.8 9.9 %collective-permute-start.25 = (bf16[192,1536]{1,0:T(8,128)(2,1)S(1)}, bf16[192,1536]{1,0:T(8,128)(2,1)S(1)}, u32[]{:S(2)}, u32[]{:S(2)}) collective-permute-start(bf16[192,1536]{1,0:T(8,128)(2,1)S(1)} %add_convert_fusion.refs_1_), channel_id=1, source_target_pairs={{0,4},{4,0},{1,5},{5,1},{2,6},{6,2},{3,7},{7,3}} | collective-permute-start | bytes 1769480 | tf_op jit(solution)/shard_map/ppermute | solution.py:319
  383.6 3.8 collective-permute-start.26
  (46 other events, 398.6 us)
Sparse Core Ops, SparseCore 0:
  28.5 22.1 all-gather.2
  67.3 20.9 all-gather.4

commit v2 on v1

v2 whole, which is shorter than its diff:
```python
import functools
import math
import jax
import jax.numpy as jnp
from jax import lax
from jax.experimental import pallas as pl
from jax.experimental.pallas import tpu as pltpu
from jax.sharding import PartitionSpec as P

RMS_EPS = 1e-6
ROPE_BASE = 10000.0
NEG_BIG = -1e30
LOG2E = 1.4426950408889634
CHUNKS = (2, 3, 3)
FF_BLOCK = 768
HEAD_BLOCK = 1024
KERNEL_MIB = 63
bf16, f32 = jnp.bfloat16, jnp.float32


def normed(x_in, gain):
    x_f = x_in.astype(f32)
    mean_sq = jnp.mean(x_f * x_f, axis=-1, keepdims=True)
    return (x_f * lax.rsqrt(mean_sq + RMS_EPS) * gain).astype(bf16)


def mm(a, b):
    return jnp.dot(a, b, preferred_element_type=f32)


def whole(shape):
    return pl.BlockSpec(shape, lambda *_: (0,) * len(shape), pipeline_mode=pl.Buffered(1))


ORDER_ONLY = pl.BlockSpec(memory_space=pl.ANY)


def call(body, flops, mib, grid, in_specs, out_shape, scratch, args, after):
    n_in, n_after = len(args), len(after)

    def run(*refs):
        body(*refs[:n_in], *refs[n_in + n_after:])

    return pl.pallas_call(
        run, grid=grid,
        in_specs=list(in_specs) + [ORDER_ONLY] * n_after,
        out_specs=[whole(o.shape) for o in out_shape], out_shape=out_shape, scratch_shapes=scratch,
        cost_estimate=pl.CostEstimate(flops=int(flops), bytes_accessed=0, transcendentals=0),
        compiler_params=pltpu.CompilerParams(vmem_limit_bytes=mib << 20),
    )(*args, *after)


def rotate(z, cos, sin):
    return (z * cos + pltpu.roll(z, z.shape[1] // 2, 1) * sin).astype(bf16)


def natural(i, rows):
    half, model = rows // 2, lax.axis_index('model')
    away = (1 - model) * half
    return i + jnp.where(i < half, away, -away)


def causal(rows):
    q = natural(lax.broadcasted_iota(jnp.int32, (rows, 1), 0), rows)
    k = natural(lax.broadcasted_iota(jnp.int32, (1, rows), 1), rows)
    return jnp.where(k <= q, 0.0, NEG_BIG)


def x_halves(xs, at, half):
    if at is not None:
        return [x[at:at + half] for x in xs]
    model = lax.axis_index('model')
    pick = lambda side: [x[pl.ds(pl.multiple_of(side * (x.shape[0] // 2), 64), x.shape[0] // 2)] for x in xs]
    return [jnp.concatenate(pick(side)) for side in (1 - model, model)]


def load_h(h, xs, at, gain):
    half = h.shape[0] // 2
    lo, hi = x_halves(xs, at, half)
    h[:half] = normed(lo, gain[...])
    h[half:] = normed(hi, gain[...])


def rope_rows(steps, base, first, rows):
    cos, sin = [], []
    sc, ss = steps[0, :rows // 2], steps[1, :rows // 2]
    for j in (first, first + 1):
        bc, bs = base[0, j:j + 1], base[1, j:j + 1]
        cos.append(bc * sc - bs * ss)
        sin.append(bs * sc + bc * ss)
    return jnp.concatenate(cos), jnp.concatenate(sin)


def layer_block(w, layer):
    return pl.BlockSpec((None,) + w.shape[1:], lambda *_: (layer,) + (0,) * (w.ndim - 1), pipeline_mode=pl.Buffered(1))


def rows_block(x, at, n):
    return pl.BlockSpec((pl.Element(n), pl.Element(x.shape[1])), lambda *_: (at, 0), pipeline_mode=pl.Buffered(1))


def prompt_body(parts, n_w, *refs):
    *xs, gain, steps, base = refs[:-3 * n_w - 2]
    ws, out, h = refs[-3 * n_w - 2:-2], refs[-2], refs[-1]
    load_h(h, xs, parts, gain)
    dim = ws[1].shape[1]
    cos, sin = rope_rows(steps, base, 0, h.shape[0])
    n_q = out.shape[1] // dim - 2 * n_w
    for i in range(0, n_q, 2):
        y = mm(h[...], jnp.concatenate([ws[0][i], ws[0][i + 1]], axis=1))
        out[:, i * dim:(i + 1) * dim] = rotate(y[:, :dim], cos, sin)
        out[:, (i + 1) * dim:(i + 2) * dim] = rotate(y[:, dim:], cos, sin)
    for i in range(n_w):
        y = mm(h[...], jnp.concatenate([ws[3 * i + 1][...], ws[3 * i + 2][...]], axis=1))
        c = (n_q + 2 * i) * dim
        out[:, c:c + dim] = rotate(y[:, :dim], cos, sin)
        out[:, c + dim:c + 2 * dim] = y[:, dim:].astype(bf16)


def prompt_qkv(xs, parts, rows, gain, ws, steps, base, with_q, after=()):
    n_heads, d_model, dim = ws[0][0][0].shape[1:]
    cols = (n_heads + 2 if with_q else 2 * len(ws)) * dim
    flat = [a for w in ws for a in w[0]]
    return call(functools.partial(prompt_body, parts, len(ws)), 4 * rows * d_model * cols, KERNEL_MIB, (1,),
                [whole(x.shape) for x in xs] + [whole(gain.shape), whole(steps.shape), whole(base.shape)] + [b for w in ws for b in w[1]],
                [jax.ShapeDtypeStruct((rows, cols), bf16)], [pltpu.VMEM((rows, d_model), bf16)],
                (*xs, gain, steps, base, *flat), after)[0]


def attend(q, kbuf, vbuf, bias):
    dim, keys, masked = q.shape[1], kbuf.shape[0], bias.shape[1]
    free = keys - masked
    s = lax.dot_general(q, kbuf[...], (((1,), (1,)), ((), ())), preferred_element_type=f32)
    diag = jnp.where(bias[...] < 0, NEG_BIG, s[:, free:])
    s = jnp.concatenate([s[:, :free], diag], axis=1) if free else diag
    top = jnp.max(s, axis=-1, keepdims=True)
    e = jnp.exp2((s - top) * (LOG2E / math.sqrt(dim)))
    p = (e * (1.0 / jnp.sum(e, axis=-1, keepdims=True))).astype(bf16)
    return mm(p, vbuf[...]).astype(bf16)


def attn_parts(n_x, n_w, parts, first, n_kv, n_seen, prompt, *refs):
    refs = list(refs)
    take = lambda n: [refs.pop(0) for _ in range(n)]
    xs = take(n_x)
    gain, steps, base = take(3)
    ws = [take(3) for _ in range(n_w)]
    pieces, seen = take(n_kv), take(n_seen)
    qkv_p = take(1)[0] if prompt else None
    out, kv_new, h, kbuf, vbuf, bias = take(6)
    bias_p = take(1)[0] if prompt else None
    rows, dim = h.shape[0], kbuf.shape[2]
    half, n_q = rows // 2, out.shape[1] // dim // n_w
    skip = qkv_p.shape[0] // 2 if prompt else 0

    def prepare():
        load_h(h, xs, parts, gain)
        bias[...] = causal(rows)
        if prompt:
            n_p, dev = qkv_p.shape[0], lax.axis_index('resp')
            bias_p[:, :n_p] = causal(n_p)
            for s in range(1, n_kv):
                bias_p[:, s * n_p:(s + 1) * n_p] = jnp.full((n_p, n_p), jnp.where(dev >= s, 0.0, NEG_BIG), f32)

    def side(m):
        wq, wk, wv = ws[m]
        cos, sin = rope_rows(steps, base, first, rows)
        fill, c = 0, 2 * m * dim
        for r in pieces + seen:
            n = r.shape[0]
            kbuf[m, fill:fill + n] = r[:, c:c + dim]
            vbuf[m, fill:fill + n] = r[:, c + dim:c + 2 * dim]
            fill += n
        y = mm(h[...], jnp.concatenate([wk[...], wv[...]], axis=1))
        k, v = rotate(y[:, :dim], cos, sin), y[:, dim:].astype(bf16)
        kv_new[:, c:c + dim], kv_new[:, c + dim:c + 2 * dim] = k, v
        kbuf[m, fill:], vbuf[m, fill:] = k, v
        if prompt:
            n_p = qkv_p.shape[0]
            for i in range(n_q):
                cols = slice(i * dim, (i + 1) * dim)
                mix = attend(qkv_p[:, cols], kbuf.at[m, :n_kv * n_p], vbuf.at[m, :n_kv * n_p], bias_p)
                out[:skip, cols] = mix[:skip]
                out[skip + half:2 * skip + half, cols] = mix[skip:]
        for i in range(0, n_q, 2):
            y = mm(h[...], jnp.concatenate([wq[i], wq[i + 1]], axis=1))
            for j in range(2):
                cols = slice((m * n_q + i + j) * dim, (m * n_q + i + j + 1) * dim)
                mix = attend(rotate(y[:, j * dim:(j + 1) * dim], cos, sin), kbuf.at[m], vbuf.at[m], bias)
                out[skip:skip + half, cols] = mix[:half]
                out[2 * skip + half:, cols] = mix[half:]

    def start():
        prepare()
        side(0)

    return [start] + [functools.partial(side, m) for m in range(1, n_w)]


def attn_body(*args):
    for part in attn_parts(*args):
        part()


def attn_chunk(xs, x_specs, parts, rows, gain, ws, steps, base, first, pieces, seen, qkv_p=None, after=()):
    d_model, dim = xs[0].shape[1], steps.shape[2]
    n_w, n_heads = len(ws), ws[0][2]
    keys = sum(a.shape[0] for a in pieces + seen) + rows
    n_p = qkv_p.shape[0] if qkv_p is not None else 0
    extra = [qkv_p] if n_p else []
    out = [jax.ShapeDtypeStruct((rows + n_p, n_w * n_heads * dim), bf16), jax.ShapeDtypeStruct((rows, 2 * n_w * dim), bf16)]
    buf = pltpu.VMEM((n_w, keys, dim), bf16)
    scratch = [pltpu.VMEM((rows, d_model), bf16), buf, buf, pltpu.VMEM((rows, rows), f32)]
    if n_p:
        scratch.append(pltpu.VMEM((n_p, n_p * len(pieces)), f32))
    rest = (*pieces, *seen, *extra)
    return call(functools.partial(attn_body, len(xs), n_w, parts, first, len(pieces), len(seen), bool(n_p)),
                n_w * (2 * rows * d_model * n_heads * dim + 8 * rows * keys * n_heads * dim), KERNEL_MIB, (1,),
                x_specs + [whole(gain.shape), whole(steps.shape), whole(base.shape)] + [b for w in ws for b in w[1]]
                + [whole(a.shape) for a in rest], out, scratch, (*xs, gain, steps, base, *[a for w in ws for a in w[0]], *rest), after)


def ffn_body(n_x, parts, layer, ff, attn, n_attn, *refs):
    refs = list(refs)
    take = lambda n: [refs.pop(0) for _ in range(n)]
    xs, gain, (wo_own, wo_far, wg, wu, wd), inputs = take(n_x), take(1)[0], take(5), take(n_attn)
    send, keep, xm = take(3)
    kv_new = take(1) if attn else []
    g, bo, bg, bu, bd, sems, *spare = refs
    step, blk, half = pl.program_id(0), bg.shape[2], send.shape[0]
    n_blk = pl.cdiv(ff, blk)
    rest = ff - (n_blk - 1) * blk
    n_pre = 1 + (attn[0] if attn else 0)

    def block_copies(j, slot, n):
        at = pl.multiple_of(j * blk, 128)
        return [pltpu.make_async_copy(wg.at[layer, :, pl.ds(at, n)], bg.at[slot, :, :n], sems.at[2 + 3 * slot]),
                pltpu.make_async_copy(wu.at[layer, :, pl.ds(at, n)], bu.at[slot, :, :n], sems.at[3 + 3 * slot]),
                pltpu.make_async_copy(wd.at[layer, pl.ds(at, n)], bd.at[slot, :n], sems.at[4 + 3 * slot])]

    @pl.when(step == 0)
    def _():
        wo_copies = [pltpu.make_async_copy(wo_own.at[layer], bo.at[0], sems.at[0]), pltpu.make_async_copy(wo_far, bo.at[1], sems.at[1])]
        for copy in wo_copies + block_copies(0, 0, blk):
            copy.start()

    if attn:
        mix, *buffers = spare
        for at, piece in enumerate(attn_parts(n_x, *attn, *xs, *inputs, mix, *kv_new, g, *buffers)):
            pl.when(step == at)(piece)

    @pl.when(step == n_pre - 1)
    def _():
        if attn:
            own, far = mix[:, :bo.shape[1]], mix[:, bo.shape[1]:]
        elif n_attn > 1:
            own, far = inputs[0][...], jnp.concatenate([inputs[1][half:], inputs[1][:half]])
        else:
            own, far = inputs[0][:, :bo.shape[1]], inputs[0][:, bo.shape[1]:]
        lo, hi = x_halves(xs, parts, half)
        wo_copies = [pltpu.make_async_copy(wo_own.at[layer], bo.at[0], sems.at[0]), pltpu.make_async_copy(wo_far, bo.at[1], sems.at[1])]
        wo_copies[0].wait()
        acc = mm(own, bo[0])
        wo_copies[1].wait()
        acc += mm(far, bo[1])
        g[:half] = normed((lo.astype(f32) + acc[:half]).astype(bf16), gain[...])
        mid = (hi.astype(f32) + acc[half:]).astype(bf16)
        xm[...] = mid
        g[half:] = normed(mid, gain[...])
        send[...] = jnp.zeros_like(send)
        keep[...] = jnp.zeros_like(keep)

    def part(slot, n):
        gate, up = mm(g[...], bg[slot, :, :n]), mm(g[...], bu[slot, :, :n])
        u = (gate * (1.0 / (1.0 + jnp.exp(-gate))) * up).astype(bf16)
        d = mm(u, bd[slot, :n])
        send[...] += d[:half]
        keep[...] += d[half:]

    j = step - n_pre
    slot = lax.rem(step + n_pre, 2)

    @pl.when((j >= 0) & (j + 1 < n_blk - 1))
    def _():
        for copy in block_copies(j + 1, 1 - slot, blk):
            copy.start()

    @pl.when(j + 1 == n_blk - 1)
    def _():
        for copy in block_copies(n_blk - 1, (n_blk - 1) % 2, rest):
            copy.start()

    @pl.when((j >= 0) & (j < n_blk - 1))
    def _():
        for copy in block_copies(j, slot, blk):
            copy.wait()
        part(slot, blk)

    @pl.when(j == n_blk - 1)
    def _():
        for copy in block_copies(n_blk - 1, (n_blk - 1) % 2, rest):
            copy.wait()
        part((n_blk - 1) % 2, rest)


def ffn_chunk(xs, x_specs, parts, layer, gain, wo_own, wo_far, wg, wu, wd, mix=None, attn=None, after=()):
    d_model, ff, blk = xs[0].shape[1], wg.shape[2], FF_BLOCK
    width = wo_far.shape[0]
    big = [pl.BlockSpec(memory_space=pl.ANY)] * 5
    flops = 6
    if attn is None:
        rows, inputs, in_specs, attn_static, spare, more = mix[0].shape[0], list(mix), [whole(a.shape) for a in mix], None, [], []
    else:
        rows, gain_a, ws, steps, base, first, pieces, seen = attn
        dim = steps.shape[2]
        keys = sum(a.shape[0] for a in pieces + seen) + rows
        inputs = [gain_a, steps, base, *[a for w in ws for a in w[0]], *pieces, *seen]
        in_specs = [whole(a.shape) for a in (gain_a, steps, base)] + [b for w in ws for b in w[1]] + [whole(a.shape) for a in pieces + seen]
        attn_static = (len(ws), parts, first, len(pieces), len(seen), False)
        buf = pltpu.VMEM((len(ws), keys, dim), bf16)
        spare = [pltpu.VMEM((rows, len(ws) * width), bf16), buf, buf, pltpu.VMEM((rows, rows), f32)]
        more = [jax.ShapeDtypeStruct((rows, 2 * len(ws) * dim), bf16)]
        flops = 8
    half = rows // 2
    out = [jax.ShapeDtypeStruct((half, d_model), f32)] * 2 + [jax.ShapeDtypeStruct((half, d_model), bf16)] + more
    scratch = [pltpu.VMEM((rows, d_model), bf16), pltpu.VMEM((2, width, d_model), bf16), pltpu.VMEM((2, d_model, blk), bf16),
               pltpu.VMEM((2, d_model, blk), bf16), pltpu.VMEM((2, blk, d_model), bf16), pltpu.SemaphoreType.DMA((8,))] + spare
    return call(functools.partial(ffn_body, len(xs), parts, layer, ff, attn_static, len(inputs)),
                flops * rows * d_model * ff, KERNEL_MIB, (1 + (attn_static[0] if attn else 0) + pl.cdiv(ff, blk),),
                x_specs + [whole(gain.shape)] + big + in_specs, out, scratch,
                (*xs, gain, wo_own, wo_far, wg, wu, wd, *inputs), after)


def head_body(row, xa, xb, gain, w, tgt, out, h, logits, top, pick):
    step, blk = pl.program_id(0), w.shape[1]

    @pl.when(step == 0)
    def _():
        load_h(h, (xa, xb), 0, gain)
        top[...] = jnp.full_like(top, NEG_BIG)
        pick[...] = jnp.zeros_like(pick)

    s = mm(h[...], w[...])
    logits[step] = s
    lanes = top.shape[1]
    hit = tgt[row:row + top.shape[0]] - step * blk
    lane = lax.broadcasted_iota(jnp.int32, top.shape, 1)
    best, found = top[...], pick[...]
    for c in range(0, blk, lanes):
        piece = s[:, c:c + lanes]
        best = jnp.maximum(best, piece)
        found += jnp.where(lane + c == hit, piece, 0.0)
    top[...], pick[...] = best, found

    @pl.when(step == pl.num_programs(0) - 1)
    def _():
        peak = jnp.max(top[...], axis=-1, keepdims=True)
        tot = jnp.zeros_like(top)
        for b in range(logits.shape[0]):
            for c in range(0, blk, lanes):
                tot += jnp.exp(logits[b, :, c:c + lanes] - peak)
        tot = jnp.sum(tot, axis=-1, keepdims=True)
        hits = jnp.sum(pick[...], axis=-1, keepdims=True)
        out[...] = jnp.where(lane == 0, peak, jnp.where(lane == 1, tot, hits))


def head_chunk(xa, xb, gain, w, tgt, row, after=()):
    d_model, vocab, blk = xa.shape[1], w.shape[1], HEAD_BLOCK
    rows = 2 * xa.shape[0]
    side = pltpu.VMEM((rows, 128), f32)
    return call(functools.partial(head_body, row), 4 * rows * d_model * vocab, KERNEL_MIB, (vocab // blk,),
                [whole(xa.shape), whole(xb.shape), whole(gain.shape), pl.BlockSpec((d_model, blk), lambda j: (0, j)), whole(tgt.shape)],
                [jax.ShapeDtypeStruct((rows, 128), f32)],
                [pltpu.VMEM((rows, d_model), bf16), pltpu.VMEM((vocab // blk, rows, blk), f32), side, side],
                (xa, xb, gain, w, tgt), after)[0]


def rope_tables(positions, head_dim):
    inv_freq = jnp.exp(jnp.arange(0, head_dim, 2, dtype=f32) * (-math.log(ROPE_BASE) / head_dim))
    angles = positions.astype(f32)[:, None] * inv_freq[None, :]
    cos, sin = jnp.cos(angles), jnp.sin(angles)
    return jnp.stack([jnp.concatenate([cos, cos], axis=1), jnp.concatenate([-sin, sin], axis=1)])


def held(x, *after):
    return lax.optimization_barrier((x, *after))[0]


def solution(mesh):
    group = mesh.shape['resp']
    rows_spec = P(('prompts', 'resp'), None)
    in_specs = (rows_spec, P(('prompts', 'resp'), None, None), rows_spec, P(), P(),
                P(None, None, 'model', None), P(None, None, 'model', None), P(None, None, 'model', None),
                P(None, 'model', None, None), P(None, None, 'model'), P(None, None, 'model'),
                P(None, 'model', None), P(), P(None, 'model'))

    def across(x):
        return lax.ppermute(x, 'model', [(0, 1), (1, 0)])

    def all_pieces(x):
        return [x] + [lax.ppermute(x, 'resp', [(i, (i + s) % group) for i in range(group)]) for s in range(1, group)]

    def local_pass(x_piece, x_own, tgt_own, attn_norm, mlp_norm, w_q, w_k, w_v, w_o, w_gate, w_up, w_down, final_norm, w_head):
        n_layers, d_model, heads_loc, dim = w_q.shape
        piece_len, resp_len = x_piece.shape[0], x_own.shape[1]
        prompt_len = piece_len * group
        dev_idx, model_idx = lax.axis_index('resp'), lax.axis_index('model')
        sizes = [resp_len * n // sum(CHUNKS) for n in CHUNKS]
        starts = [sum(sizes[:c]) for c in range(len(sizes))]
        n_chunks = len(sizes)

        def joined(part):
            return lax.all_gather(part, 'resp', axis=0, tiled=True)

        w_out = w_o.reshape(n_layers, heads_loc * dim, d_model)
        part = heads_loc * dim // group

        def wo_part(l, *after):
            x = lax.dynamic_slice(w_out, (l, dev_idx * part, 0), (1, part, d_model))[0]
            return across(held(x, *after))

        def own_heads(l, *after):
            w = (held(w_q, *after)[l].transpose(1, 0, 2)[None], w_k[l].reshape(1, d_model, dim), w_v[l].reshape(1, d_model, dim))
            return w, [layer_block(a, 0) for a in w], heads_loc

        def far_heads(w):
            spec = lambda n, i: pl.BlockSpec((n, d_model, dim), lambda *_: (i, 0, 0), pipeline_mode=pl.Buffered(1))
            return (w, w, w), [spec(heads_loc, 0), spec(None, heads_loc), spec(None, heads_loc + 1)], heads_loc

        def halves(x, at, n):
            half = n // 2
            return (lax.dynamic_slice_in_dim(x, at + (1 - model_idx) * half, half, 0),
                    lax.dynamic_slice_in_dim(x, at + model_idx * half, half, 0))

        steps = rope_tables(jnp.arange(max(sizes) // 2), dim)
        both = jnp.stack([1 - model_idx, model_idx])
        base = rope_tables(jnp.concatenate([dev_idx * piece_len + both * (piece_len // 2)] + [
            prompt_len + at + both * (n // 2) for at, n in zip(starts, sizes)]), dim)
        x_rows = x_own[0]

        def source(l, c, with_prompt):
            if l == 0:
                xs = ([x_piece] if with_prompt else []) + [x_rows]
                return xs, ([whole(x_piece.shape)] if with_prompt else []) + [rows_block(x_rows, starts[c], sizes[c])], None
            return x_r[c], [whole(x.shape) for x in x_r[c]], 0 if c else piece_len // 2

        x_r, far = {}, {}
        pending = {}

        def mlp_of(l, c, wo_far, after, mix=None, attn=None):
            xs, specs, parts = source(l, c, c == 0)
            *pending[c], = ffn_chunk(xs, specs, parts, l, mlp_norm[l][None], w_out, wo_far, w_gate, w_up, w_down, mix, attn, after)
            return pending[c][1]

        def send(c, *after):
            far[c] = across(held(pending[c][0], *after))

        def collect(c, *after):
            _, keep, xm = pending.pop(c)[:3]
            mine = (xm.astype(f32) + (keep + held(far.pop(c), *after))).astype(bf16)
            x_r[c] = [across(mine), mine]
            return mine

        end = n_chunks - 1
        gain = attn_norm[0][None]
        w_own = own_heads(0)
        qkv_p = prompt_qkv([x_piece], None, piece_len, gain, [w_own], steps, base, True)
        pieces = all_pieces(qkv_p[:, heads_loc * dim:])
        wo_sent = [wo_part(0, qkv_p)]
        w_next = own_heads(1, qkv_p)
        heads = jnp.concatenate([w_next[0][0][0], w_next[0][1], w_next[0][2]])
        per = heads.shape[0] // group
        w_part = across(lax.dynamic_slice_in_dim(heads, dev_idx * per, per, 0))
        a, seen, tail = [], [], ()
        for c in range(n_chunks):
            xs, specs, parts = source(0, c, False)
            mix, kv = attn_chunk(xs, specs, parts, sizes[c], gain, [w_own], steps, base, 2 + 2 * c, pieces, list(seen),
                                 qkv_p if c == 0 else None, tail)
            seen.append(kv)
            a.append((mix, across(mix)))
            tail = (mix,)
            if c == 0:
                wo_far = [joined(held(wo_sent[0], mix))]
        wo_sent.append(wo_part(1, a[-1][0]))
        for c in range(n_chunks):
            tail = (mlp_of(0, c, wo_far[0], tail, mix=a[c]),)
            if c == 0:
                w_far = far_heads(joined(held(w_part, *tail)))
                send(c)
            elif c < end or c == 1:
                tail = (*tail, collect(c - 1, *tail))
                if c < end:
                    send(c)
            if c == 1:
                wo_far.append(joined(held(wo_sent[1], *tail)))
        gain = attn_norm[1][None]
        both_w = [w_next, w_far]
        kv_p = prompt_qkv(x_r[0], 0, piece_len, gain, both_w, steps, base, False, tail)
        pieces = all_pieces(kv_p)
        tail = (kv_p, collect(end - 1, kv_p)) if end > 1 else (kv_p,)
        send(end)
        seen = []
        tail = (mlp_of(1, 0, wo_far[1], tail, attn=(sizes[0], gain, both_w, steps, base, 2, pieces, [])),)
        seen.append(pending[0][3])
        tail = (*tail, collect(end, *tail))
        send(0)

        def attention(c, ws, after):
            xs, specs, parts = source(1, c, False)
            mix, kv = attn_chunk(xs, specs, parts, sizes[c], gain, ws, steps, base, 2 + 2 * c, pieces, list(seen), None, after)
            seen.append(kv)
            return mix

        mixes = {}
        for c in range(1, n_chunks):
            mix = attention(c, both_w if c < end else both_w[:1], tail)
            mixes[c] = [mix] if c < end else [mix, across(mix)]
            tail = (mix,)
        for c in range(1, n_chunks):
            if c < end:
                tail = (*tail, collect(c - 1, *tail))
            tail = (mlp_of(1, c, wo_far[1], tail, mix=mixes[c]),)
            if c == end:
                collect(c - 1, *tail)
            send(c)
        tgt = tgt_own[0] - model_idx * w_head.shape[1]
        tgt = held(jnp.concatenate([h for at, n in zip(starts, sizes) for h in halves(tgt, at, n)]), *tail)[:, None]
        stats = []
        for c in range(n_chunks):
            if c == end:
                collect(c, *tail)
            out = head_chunk(*x_r[c], final_norm[None], w_head, tgt, starts[c], tail)
            tail = (out,)
            stats.append(jnp.concatenate(halves(out[:, :3], 0, sizes[c])))
        here = jnp.concatenate(stats).T
        there = across(here)
        top = jnp.maximum(here[0], there[0])
        tot = here[1] * jnp.exp(here[0] - top) + there[1] * jnp.exp(there[0] - top)
        logp = here[2] + there[2] - top - jnp.log(tot)
        return logp[None, :]

    return jax.shard_map(local_pass, mesh=mesh, in_specs=in_specs, out_specs=rows_spec, check_vma=False)
```

time: 399 us -> 459 us (1.15)
  waiting for transfers between devices: 57.3 us -> 101 us
  Pallas kernels: 248 us -> 270 us
  local copies, waits for them, and re-layouts: 34.4 us -> 22.4 us
  other arithmetic: 8.77 us -> 16.9 us
    ppermute x21 -> x20, waiting for transfers between devices: 57.2 us -> 97.1 us  [across(): return lax.ppermute(x, 'model', [(0, 1), (1, 0)])]
    pallas_call x17 -> x16, Pallas kernels: 248 us -> 270 us  [call(): pl.pallas_call(run, grid=grid, in_specs=list(in_specs) + [ORDER_ONLY] * n...]
    unnamed x98 -> x50, local copies, waits for them, and re-layouts: 13.7 us -> 3.9 us
    convert_element_type x6, other arithmetic: 6.52 us -> 12.7 us  [collect(): mine = (xm.astype(f32) + (keep + held(far.pop(c), *after))).astype(bf16)]
    ppermute x21 -> x20, starting transfers between devices: 25.5 us -> 20.8 us  [across(): return lax.ppermute(x, 'model', [(0, 1), (1, 0)])]
  transfers between devices with their start and end apart: 29 -> 29, of which waited for: 8 -> 13; matrix products, arithmetic and copies ran while one was open for 6% -> 5% of each run, Pallas kernels for 60% -> 56%
where the time goes in v2:
time: 459 us; the launch traced here: 453 us
  Pallas kernels  270 us (59%)
  waiting for transfers between devices  101 us (22%)
  starting transfers between devices  28.1 us (6%)
  local copies, waits for them, and re-layouts  22.4 us (5%)
  other arithmetic  16.9 us (4%)
  between operations  13.8 us (3%)
    pallas_call x16, Pallas kernels, call(): pl.pallas_call(run, grid=grid, in_specs=list(in_specs) + [ORDER_ONLY] * n...  270 us
    ppermute x20, waiting for transfers between devices, across(): return lax.ppermute(x, 'model', [(0, 1), (1, 0)])  97.1 us
    ppermute x20, starting transfers between devices, across(): return lax.ppermute(x, 'model', [(0, 1), (1, 0)])  20.8 us
    convert_element_type x6, other arithmetic, collect(): mine = (xm.astype(f32) + (keep + held(far.pop(c), *after))).astype(bf16)  12.7 us
  transfers between devices with their start and end apart: 29, of which 13 were waited for; matrix products, arithmetic and copies ran while one was open for 5% of the time, Pallas kernels for 56%

profile of v2, /device:TPU:0, one launch (start us, length us, event | category | flops | bytes accessed | tf_op | source)
XLA Modules:
  0.0 453.0 jit_solution(9769943121580148617)
XLA Ops:
  8.7 3.4 slice_bitcast_fusion.refs_4_
  14.6 2.6 dynamic-slice_bitcast_fusion
  17.2 3.5 shard_map.136.refs_11_
  20.7 3.3 collective-permute-start
  30.4 10.7 %shard_map.137 = (bf16[384,768]{1,0:T(8,128)(2,1)}, bf16[256,256]{1,0:T(8,128)(2,1)}) custom-call(bf16[1024,1536]{1,0:T(8,128)(2,1)} %bitcast.57, f32[1,1536]{1,0:T(1,128)} %get-tuple-element.102.refs_1_, f32[2,192,128]{2,1,0:T(8,128)} %pad_maximum_fusion.refs_2_.refs_3_.refs_9_, f32[2,8,128]{2,1,0:T(8,128)} %pad_maximum_fusion.1.refs_3_.refs_4_.refs_10_, ...), custom_call_target="tpu_custom_call" | custom-call | flops 1811939328 | tf_op jit(solution)/shard_map/pallas_call | solution.py:44
  41.7 3.9 slice_bitcast_fusion.2
  49.7 11.5 %shard_map.138 = (bf16[384,768]{1,0:T(8,128)(2,1)}, bf16[384,256]{1,0:T(8,128)(2,1)}) custom-call(bf16[1024,1536]{1,0:T(8,128)(2,1)} %bitcast.58, f32[1,1536]{1,0:T(1,128)} %get-tuple-element.102.refs_1_, f32[2,192,128]{2,1,0:T(8,128)} %pad_maximum_fusion.refs_2_.refs_3_.refs_9_, f32[2,8,128]{2,1,0:T(8,128)} %pad_maximum_fusion.1.refs_3_.refs_4_.refs_10_, ...), custom_call_target="tpu_custom_call" | custom-call | flops 3623878656 | tf_op jit(solution)/shard_map/pallas_call | solution.py:44
  61.2 11.8 %shard_map.139 = (bf16[384,768]{1,0:T(8,128)(2,1)}, bf16[384,256]{1,0:T(8,128)(2,1)}) custom-call(bf16[1024,1536]{1,0:T(8,128)(2,1)} %bitcast.59, f32[1,1536]{1,0:T(1,128)} %get-tuple-element.102.refs_1_, f32[2,192,128]{2,1,0:T(8,128)} %pad_maximum_fusion.refs_2_.refs_3_.refs_9_, f32[2,8,128]{2,1,0:T(8,128)} %pad_maximum_fusion.1.refs_3_.refs_4_.refs_10_, ...), custom_call_target="tpu_custom_call" | custom-call | flops 4529848320 | tf_op jit(solution)/shard_map/pallas_call | solution.py:44
  73.0 7.2 %collective-permute-done.4.refs_9_ = bf16[384,768]{1,0:T(8,128)(2,1)} collective-permute-done((bf16[384,768]{1,0:T(8,128)(2,1)}, bf16[384,768]{1,0:T(8,128)(2,1)}, u32[]{:S(2)}, u32[]{:S(2)}) %collective-permute-start.4) | collective-permute-done | bytes 589856 | tf_op jit(solution)/shard_map/ppermute | solution.py:398
  80.2 26.2 %shard_map.140 = (f32[192,1536]{1,0:T(8,128)}, f32[192,1536]{1,0:T(8,128)}, bf16[192,1536]{1,0:T(8,128)(2,1)}) custom-call(bf16[128,1536]{1,0:T(8,128)(2,1)} %refs_0_.3, bf16[1024,1536]{1,0:T(8,128)(2,1)} %bitcast.60, f32[1,1536]{1,0:T(1,128)} %get-tuple-element.104.refs_2_.refs_1_, bf16[2,768,1536]{2,1,0:T(8,128)(2,1)} %bitcast.51, ...), custom_call_target="tpu_custom_call" | custom-call | flops 15854469120 | tf_op jit(solution)/shard_map/pallas_call | solution.py:44
  110.6 13.7 %collective-permute-done.6.refs_8_ = bf16[384,768]{1,0:T(8,128)(2,1)S(1)} collective-permute-done((bf16[384,768]{1,0:T(8,128)(2,1)}, bf16[384,768]{1,0:T(8,128)(2,1)S(1)}, u32[]{:S(2)}, u32[]{:S(2)}) %collective-permute-start.6) | collective-permute-done | bytes 589856 | tf_op jit(solution)/shard_map/ppermute | solution.py:398
  125.1 26.3 %shard_map.141 = (f32[192,1536]{1,0:T(8,128)}, f32[192,1536]{1,0:T(8,128)}, bf16[192,1536]{1,0:T(8,128)(2,1)}) custom-call(bf16[1024,1536]{1,0:T(8,128)(2,1)} %bitcast.61, f32[1,1536]{1,0:T(1,128)} %get-tuple-element.104.refs_2_.refs_1_, bf16[2,768,1536]{2,1,0:T(8,128)(2,1)} %bitcast.52, bf16[768,1536]{1,0:T(8,128)(2,1)} %all-gather.4.cloned.1.call-done.refs_4_.refs_3_, ...), custom_call_target="tpu_custom_call" | custom-call | flops 15854469120 | tf_op jit(solution)/shard_map/pallas_call | solution.py:44
  151.4 10.0 %collective-permute-done.5 = f32[192,1536]{1,0:T(8,128)} collective-permute-done((f32[192,1536]{1,0:T(8,128)}, f32[192,1536]{1,0:T(8,128)}, u32[]{:S(2)}, u32[]{:S(2)}) %collective-permute-start.5) | collective-permute-done | bytes 1179680 | tf_op jit(solution)/shard_map/ppermute | solution.py:398
  161.4 2.1 add_convert_fusion.4.refs_10_.refs_1_
  167.7 12.2 %collective-permute-done.10.refs_8_ = bf16[384,768]{1,0:T(8,128)(2,1)} collective-permute-done((bf16[384,768]{1,0:T(8,128)(2,1)S(1)}, bf16[384,768]{1,0:T(8,128)(2,1)}, u32[]{:S(2)}, u32[]{:S(2)}) %collective-permute-start.10) | collective-permute-done | bytes 589856 | tf_op jit(solution)/shard_map/ppermute | solution.py:398
  179.9 26.2 %shard_map.142 = (f32[192,1536]{1,0:T(8,128)}, f32[192,1536]{1,0:T(8,128)}, bf16[192,1536]{1,0:T(8,128)(2,1)}) custom-call(bf16[1024,1536]{1,0:T(8,128)(2,1)} %bitcast.62, f32[1,1536]{1,0:T(1,128)} %get-tuple-element.104.refs_2_.refs_1_, bf16[2,768,1536]{2,1,0:T(8,128)(2,1)} %bitcast.53, bf16[768,1536]{1,0:T(8,128)(2,1)} %all-gather.4.cloned.1.call-done.refs_4_.refs_3_, ...), custom_call_target="tpu_custom_call" | custom-call | flops 15854469120 | tf_op jit(solution)/shard_map/pallas_call | solution.py:44
  206.9 10.9 %collective-permute-done.7.refs_0_ = bf16[192,1536]{1,0:T(8,128)(2,1)} collective-permute-done((bf16[192,1536]{1,0:T(8,128)(2,1)S(1)}, bf16[192,1536]{1,0:T(8,128)(2,1)}, u32[]{:S(2)}, u32[]{:S(2)}) %collective-permute-start.7) | collective-permute-done | bytes 589856 | tf_op jit(solution)/shard_map/ppermute | solution.py:398
  217.8 4.4 shard_map.143.refs_17_.refs_21_.refs_11_.refs_8_
  225.5 2.0 add_convert_fusion.3.refs_22_.refs_1_
  231.2 33.4 %shard_map.144 = (f32[128,1536]{1,0:T(8,128)}, f32[128,1536]{1,0:T(8,128)}, bf16[128,1536]{1,0:T(8,128)(2,1)}, bf16[256,512]{1,0:T(8,128)(2,1)}) custom-call(bf16[192,1536]{1,0:T(8,128)(2,1)} %collective-permute-done.7.refs_0_, bf16[192,1536]{1,0:T(8,128)(2,1)} %copy-done, f32[1,1536]{1,0:T(1,128)} %get-tuple-element.103.refs_2_, ...), custom_call_target="tpu_custom_call" | custom-call | flops 14092861440 | tf_op jit(solution)/shard_map/pallas_call | solution.py:44
  264.6 2.9 add_convert_fusion.2.refs_17_.refs_1_
  269.5 20.8 %shard_map.145 = (bf16[384,1536]{1,0:T(8,128)(2,1)}, bf16[384,512]{1,0:T(8,128)(2,1)}) custom-call(bf16[192,1536]{1,0:T(8,128)(2,1)} %collective-permute-done.18.refs_0_, bf16[192,1536]{1,0:T(8,128)(2,1)} %copy-done.3, f32[1,1536]{1,0:T(1,128)} %get-tuple-element.101.refs_2_.refs_8_, f32[2,192,128]{2,1,0:T(8,128)} %pad_maximum_fusion.refs_2_.refs_3_.refs_9_, ...), custom_call_target="tpu_custom_call" | custom-call | flops 7247757312 | tf_op jit(solution)/shard_map/pallas_call | solution.py:44
  290.3 11.8 %shard_map.146 = (bf16[384,768]{1,0:T(8,128)(2,1)}, bf16[384,256]{1,0:T(8,128)(2,1)}) custom-call(bf16[192,1536]{1,0:T(8,128)(2,1)} %collective-permute-done.17.refs_0_, bf16[192,1536]{1,0:T(8,128)(2,1)} %add_convert_fusion.2.refs_17_.refs_1_, f32[1,1536]{1,0:T(1,128)} %get-tuple-element.101.refs_2_.refs_8_, ...), custom_call_target="tpu_custom_call" | custom-call | flops 4529848320 | tf_op jit(solution)/shard_map/pallas_call | solution.py:44
  305.8 26.3 %shard_map.147 = (f32[192,1536]{1,0:T(8,128)}, f32[192,1536]{1,0:T(8,128)}, bf16[192,1536]{1,0:T(8,128)(2,1)}) custom-call(bf16[192,1536]{1,0:T(8,128)(2,1)} %collective-permute-done.18.refs_0_, bf16[192,1536]{1,0:T(8,128)(2,1)} %copy-done.3, f32[1,1536]{1,0:T(1,128)} %get-tuple-element.103.refs_2_, bf16[2,768,1536]{2,1,0:T(8,128)(2,1)} %bitcast.55, ...), custom_call_target="tpu_custom_call" | custom-call | flops 15854469120 | tf_op jit(solution)/shard_map/pallas_call | solution.py:44
  333.6 26.4 %shard_map.148 = (f32[192,1536]{1,0:T(8,128)}, f32[192,1536]{1,0:T(8,128)}, bf16[192,1536]{1,0:T(8,128)(2,1)}) custom-call(bf16[192,1536]{1,0:T(8,128)(2,1)} %collective-permute-done.17.refs_0_, bf16[192,1536]{1,0:T(8,128)(2,1)} %add_convert_fusion.2.refs_17_.refs_1_, f32[1,1536]{1,0:T(1,128)} %get-tuple-element.103.refs_2_, bf16[2,768,1536]{2,1,0:T(8,128)(2,1)} %bitcast.56, ...), custom_call_target="tpu_custom_call" | custom-call | flops 15854469120 | tf_op jit(solution)/shard_map/pallas_call | solution.py:44
  365.8 9.1 %shard_map.149.refs_5_ = f32[256,128]{1,0:T(8,128)} custom-call(bf16[128,1536]{1,0:T(8,128)(2,1)} %collective-permute-done.19.refs_0_, bf16[128,1536]{1,0:T(8,128)(2,1)} %copy-done.5, f32[1,1536]{1,0:T(1,128)} %broadcast_in_dim.10.refs_2_, bf16[1536,4096]{1,0:T(8,128)(2,1)} %refs_3_.5, s32[1024,1]{1,0:T(8,128)} %copy.20.refs_4_, ...), custom_call_target="tpu_custom_call" | custom-call | flops 6442450944 | tf_op jit(solution)/shard_map/pallas_call | solution.py:44
  374.9 27.3 %collective-permute-done.22.refs_0_ = bf16[192,1536]{1,0:T(8,128)(2,1)} collective-permute-done((bf16[192,1536]{1,0:T(8,128)(2,1)S(1)}, bf16[192,1536]{1,0:T(8,128)(2,1)}, u32[]{:S(2)}, u32[]{:S(2)}) %collective-permute-start.22) | collective-permute-done | bytes 589856 | tf_op jit(solution)/shard_map/ppermute | solution.py:398
  402.2 10.8 %shard_map.150.refs_5_ = f32[384,128]{1,0:T(8,128)} custom-call(bf16[192,1536]{1,0:T(8,128)(2,1)} %collective-permute-done.22.refs_0_, bf16[192,1536]{1,0:T(8,128)(2,1)} %copy-done.11, f32[1,1536]{1,0:T(1,128)} %broadcast_in_dim.10.refs_2_, bf16[1536,4096]{1,0:T(8,128)(2,1)} %refs_3_.5, s32[1024,1]{1,0:T(8,128)} %copy.20.refs_4_, f32[256,128]{1,0:T(8,128)} %shard_map.149.refs_5_), custom_call_target="tpu_custom_call" | custom-call | flops 9663676416 | tf_op jit(solution)/shard_map/pallas_call | solution.py:44
  413.1 2.1 add_convert_fusion.refs_1_
  416.6 12.8 %collective-permute-done.24.refs_0_ = bf16[192,1536]{1,0:T(8,128)(2,1)} collective-permute-done((bf16[192,1536]{1,0:T(8,128)(2,1)S(1)}, bf16[192,1536]{1,0:T(8,128)(2,1)}, u32[]{:S(2)}, u32[]{:S(2)}) %collective-permute-start.24) | collective-permute-done | bytes 589856 | tf_op jit(solution)/shard_map/ppermute | solution.py:398
  429.3 11.1 %shard_map.151 = f32[384,128]{1,0:T(8,128)} custom-call(bf16[192,1536]{1,0:T(8,128)(2,1)} %collective-permute-done.24.refs_0_, bf16[192,1536]{1,0:T(8,128)(2,1)} %copy-done.10, f32[1,1536]{1,0:T(1,128)} %broadcast_in_dim.10.refs_2_, bf16[1536,4096]{1,0:T(8,128)(2,1)} %refs_3_.5, s32[1024,1]{1,0:T(8,128)} %copy.20.refs_4_, f32[384,128]{1,0:T(8,128)} %shard_map.150.refs_5_), custom_call_target="tpu_custom_call" | custom-call | flops 9663676416 | tf_op jit(solution)/shard_map/pallas_call | solution.py:44
  442.4 3.0 collective-permute-done.25
  (137 shorter events, 49.4 us)
Async XLA Ops:
  6.5 73.7 %all-gather.4.cloned.1.call-start = ((), (), s32[]{:S(2)}) async-start(), calls=%async_computation | async-start | bytes 2949120 | tf_op jit(solution)/shard_map/all_gather | solution.py:413
  14.6 31.1 %copy-start.1 = (bf16[1,1536,128]{2,1,0:T(8,128)(2,1)}, bf16[1,1536,128]{2,1,0:T(8,128)(2,1)S(1)}, u32[]{:S(2)}) copy-start(bf16[1,1536,128]{2,1,0:T(8,128)(2,1)S(1)} %get-tuple-element.91.refs_7_.refs_13_) | copy-start | bytes 1179652
  14.6 31.1 %copy-start.2 = (bf16[1,1536,128]{2,1,0:T(8,128)(2,1)}, bf16[1,1536,128]{2,1,0:T(8,128)(2,1)S(1)}, u32[]{:S(2)}) copy-start(bf16[1,1536,128]{2,1,0:T(8,128)(2,1)S(1)} %get-tuple-element.125.refs_6_.refs_12_) | copy-start | bytes 1179652
  20.7 20.4 %collective-permute-start = (bf16[192,1536]{1,0:T(8,128)(2,1)}, bf16[192,1536]{1,0:T(8,128)(2,1)}, u32[]{:S(2)}, u32[]{:S(2)}) collective-permute-start(bf16[192,1536]{1,0:T(8,128)(2,1)} %get-tuple-element.45), channel_id=1, source_target_pairs={{0,4},{4,0},{1,5},{5,1},{2,6},{6,2},{3,7},{7,3}} | collective-permute-start | bytes 1769480 | tf_op jit(solution)/shard_map/ppermute | solution.py:398
  24.9 3.8 collective-permute-start.1
  24.9 4.6 %collective-permute-start.2 = (bf16[128,256]{1,0:T(8,128)(2,1)S(1)}, bf16[128,256]{1,0:T(8,128)(2,1)S(1)}, u32[]{:S(2)}, u32[]{:S(2)}) collective-permute-start(bf16[128,256]{1,0:T(8,128)(2,1)S(1)} %slice.87.refs_7_), channel_id=1, source_target_pairs={{0,2},{1,3},{2,0},{3,1},{4,6},{5,7},{6,4},{7,5}} | collective-permute-start | bytes 196616 | tf_op jit(solution)/shard_map/ppermute | solution.py:401
  26.4 3.3 collective-permute-start.3
  41.1 176.7 %all-gather.8.cloned.1.call-start = ((), (), s32[]{:S(2)}) async-start(), calls=%async_computation.2 | async-start | bytes 3932160 | tf_op jit(solution)/shard_map/all_gather | solution.py:413
  47.0 59.4 %collective-permute-start.9 = (bf16[2,1536,128]{2,1,0:T(8,128)(2,1)}, bf16[2,1536,128]{2,1,0:T(8,128)(2,1)S(1)}, u32[]{:S(2)}, u32[]{:S(2)}) collective-permute-start(bf16[2,1536,128]{2,1,0:T(8,128)(2,1)} %fusion.1), channel_id=1, source_target_pairs={{0,4},{4,0},{1,5},{5,1},{2,6},{6,2},{3,7},{7,3}} | collective-permute-start | bytes 2359304 | tf_op jit(solution)/shard_map/ppermute | solution.py:398
  48.1 32.1 %collective-permute-start.4 = (bf16[384,768]{1,0:T(8,128)(2,1)}, bf16[384,768]{1,0:T(8,128)(2,1)}, u32[]{:S(2)}, u32[]{:S(2)}) collective-permute-start(bf16[384,768]{1,0:T(8,128)(2,1)} %get-tuple-element.46.refs_12_.refs_8_), channel_id=1, source_target_pairs={{0,4},{4,0},{1,5},{5,1},{2,6},{6,2},{3,7},{7,3}} | collective-permute-start | bytes 1769480 | tf_op jit(solution)/shard_map/ppermute | solution.py:398
  107.4 120.7 %all-gather.6.cloned.1.call-start = ((), (), s32[]{:S(2)}) async-start(), calls=%async_computation.1 | async-start | bytes 2949120 | tf_op jit(solution)/shard_map/all_gather | solution.py:413
  107.8 16.4 %collective-permute-start.6 = (bf16[384,768]{1,0:T(8,128)(2,1)}, bf16[384,768]{1,0:T(8,128)(2,1)S(1)}, u32[]{:S(2)}, u32[]{:S(2)}) collective-permute-start(bf16[384,768]{1,0:T(8,128)(2,1)} %get-tuple-element.50.refs_13_.refs_7_), channel_id=1, source_target_pairs={{0,4},{4,0},{1,5},{5,1},{2,6},{6,2},{3,7},{7,3}} | collective-permute-start | bytes 1769480 | tf_op jit(solution)/shard_map/ppermute | solution.py:398
  108.5 55.0 %collective-permute-start.8 = (bf16[192,1536]{1,0:T(8,128)(2,1)}, bf16[192,1536]{1,0:T(8,128)(2,1)}, u32[]{:S(2)}, u32[]{:S(2)}) collective-permute-start(bf16[192,1536]{1,0:T(8,128)(2,1)} %get-tuple-element.57), channel_id=1, source_target_pairs={{0,4},{4,0},{1,5},{5,1},{2,6},{6,2},{3,7},{7,3}} | collective-permute-start | bytes 1769480 | tf_op jit(solution)/shard_map/ppermute | solution.py:398
  109.9 51.6 %collective-permute-start.5 = (f32[192,1536]{1,0:T(8,128)}, f32[192,1536]{1,0:T(8,128)}, u32[]{:S(2)}, u32[]{:S(2)}) collective-permute-start(f32[192,1536]{1,0:T(8,128)} %get-tuple-element.54), channel_id=1, source_target_pairs={{0,4},{4,0},{1,5},{5,1},{2,6},{6,2},{3,7},{7,3}} | collective-permute-start | bytes 3538952 | tf_op jit(solution)/shard_map/ppermute | solution.py:398
  163.5 16.4 %copy-start = (bf16[192,1536]{1,0:T(8,128)(2,1)}, bf16[192,1536]{1,0:T(8,128)(2,1)S(1)}, u32[]{:S(2)}) copy-start(bf16[192,1536]{1,0:T(8,128)(2,1)S(1)} %add_convert_fusion.4.refs_10_.refs_1_) | copy-start | bytes 1769476
  163.6 16.3 %collective-permute-start.10 = (bf16[384,768]{1,0:T(8,128)(2,1)S(1)}, bf16[384,768]{1,0:T(8,128)(2,1)}, u32[]{:S(2)}, u32[]{:S(2)}) collective-permute-start(bf16[384,768]{1,0:T(8,128)(2,1)S(1)} %copy-done.4), channel_id=1, source_target_pairs={{0,4},{4,0},{1,5},{5,1},{2,6},{6,2},{3,7},{7,3}} | collective-permute-start | bytes 1769480 | tf_op jit(solution)/shard_map/ppermute | solution.py:398
  165.7 59.8 %collective-permute-start.14 = (f32[192,1536]{1,0:T(8,128)}, f32[192,1536]{1,0:T(8,128)}, u32[]{:S(2)}, u32[]{:S(2)}) collective-permute-start(f32[192,1536]{1,0:T(8,128)} %get-tuple-element.63), channel_id=1, source_target_pairs={{0,4},{4,0},{1,5},{5,1},{2,6},{6,2},{3,7},{7,3}} | collective-permute-start | bytes 3538952 | tf_op jit(solution)/shard_map/ppermute | solution.py:398
  167.0 50.8 %collective-permute-start.7 = (bf16[192,1536]{1,0:T(8,128)(2,1)S(1)}, bf16[192,1536]{1,0:T(8,128)(2,1)}, u32[]{:S(2)}, u32[]{:S(2)}) collective-permute-start(bf16[192,1536]{1,0:T(8,128)(2,1)S(1)} %add_convert_fusion.4.refs_10_.refs_1_), channel_id=1, source_target_pairs={{0,4},{4,0},{1,5},{5,1},{2,6},{6,2},{3,7},{7,3}} | collective-permute-start | bytes 1769480 | tf_op jit(solution)/shard_map/ppermute | solution.py:398
  206.1 58.5 %collective-permute-start.16 = (f32[192,1536]{1,0:T(8,128)}, f32[192,1536]{1,0:T(8,128)}, u32[]{:S(2)}, u32[]{:S(2)}) collective-permute-start(f32[192,1536]{1,0:T(8,128)} %get-tuple-element.69), channel_id=1, source_target_pairs={{0,4},{4,0},{1,5},{5,1},{2,6},{6,2},{3,7},{7,3}} | collective-permute-start | bytes 3538952 | tf_op jit(solution)/shard_map/ppermute | solution.py:398
  222.2 5.8 %collective-permute-start.11 = (bf16[128,512]{1,0:T(8,128)(2,1)}, bf16[128,512]{1,0:T(8,128)(2,1)S(1)}, u32[]{:S(2)}, u32[]{:S(2)}) collective-permute-start(bf16[128,512]{1,0:T(8,128)(2,1)} %shard_map.143.refs_17_.refs_21_.refs_11_.refs_8_), channel_id=1, source_target_pairs={{0,1},{1,2},{2,3},{3,0},{4,5},{5,6},{6,7},{7,4}} | collective-permute-start | bytes 393224 | tf_op jit(solution)/shard_map/ppermute | solution.py:401
  222.2 6.6 %collective-permute-start.12 = (bf16[128,512]{1,0:T(8,128)(2,1)}, bf16[128,512]{1,0:T(8,128)(2,1)S(1)}, u32[]{:S(2)}, u32[]{:S(2)}) collective-permute-start(bf16[128,512]{1,0:T(8,128)(2,1)} %shard_map.143.refs_17_.refs_21_.refs_11_.refs_8_), channel_id=1, source_target_pairs={{0,2},{1,3},{2,0},{3,1},{4,6},{5,7},{6,4},{7,5}} | collective-permute-start | bytes 393224 | tf_op jit(solution)/shard_map/ppermute | solution.py:401
  224.0 6.4 %collective-permute-start.13 = (bf16[128,512]{1,0:T(8,128)(2,1)}, bf16[128,512]{1,0:T(8,128)(2,1)S(1)}, u32[]{:S(2)}, u32[]{:S(2)}) collective-permute-start(bf16[128,512]{1,0:T(8,128)(2,1)} %shard_map.143.refs_17_.refs_21_.refs_11_.refs_8_), channel_id=1, source_target_pairs={{0,3},{1,0},{2,1},{3,2},{4,7},{5,4},{6,5},{7,6}} | collective-permute-start | bytes 393224 | tf_op jit(solution)/shard_map/ppermute | solution.py:401
  227.5 42.0 %collective-permute-start.18 = (bf16[192,1536]{1,0:T(8,128)(2,1)S(1)}, bf16[192,1536]{1,0:T(8,128)(2,1)}, u32[]{:S(2)}, u32[]{:S(2)}) collective-permute-start(bf16[192,1536]{1,0:T(8,128)(2,1)S(1)} %add_convert_fusion.3.refs_22_.refs_1_), channel_id=1, source_target_pairs={{0,4},{4,0},{1,5},{5,1},{2,6},{6,2},{3,7},{7,3}} | collective-permute-start | bytes 1769480 | tf_op jit(solution)/shard_map/ppermute | solution.py:398
  267.5 22.8 %collective-permute-start.17 = (bf16[192,1536]{1,0:T(8,128)(2,1)}, bf16[192,1536]{1,0:T(8,128)(2,1)}, u32[]{:S(2)}, u32[]{:S(2)}) collective-permute-start(bf16[192,1536]{1,0:T(8,128)(2,1)} %add_convert_fusion.2.refs_17_.refs_1_), channel_id=1, source_target_pairs={{0,4},{4,0},{1,5},{5,1},{2,6},{6,2},{3,7},{7,3}} | collective-permute-start | bytes 1769480 | tf_op jit(solution)/shard_map/ppermute | solution.py:398
  268.0 34.6 %collective-permute-start.15 = (f32[128,1536]{1,0:T(8,128)}, f32[128,1536]{1,0:T(8,128)}, u32[]{:S(2)}, u32[]{:S(2)}) collective-permute-start(f32[128,1536]{1,0:T(8,128)} %get-tuple-element.67), channel_id=1, source_target_pairs={{0,4},{4,0},{1,5},{5,1},{2,6},{6,2},{3,7},{7,3}} | collective-permute-start | bytes 2359304 | tf_op jit(solution)/shard_map/ppermute | solution.py:398
  302.1 30.7 %collective-permute-start.20 = (bf16[384,768]{1,0:T(8,128)(2,1)}, bf16[384,768]{1,0:T(8,128)(2,1)S(1)}, u32[]{:S(2)}, u32[]{:S(2)}) collective-permute-start(bf16[384,768]{1,0:T(8,128)(2,1)} %get-tuple-element.74.refs_9_.refs_8_), channel_id=1, source_target_pairs={{0,4},{4,0},{1,5},{5,1},{2,6},{6,2},{3,7},{7,3}} | collective-permute-start | bytes 1769480 | tf_op jit(solution)/shard_map/ppermute | solution.py:398
  304.2 61.6 %collective-permute-start.19 = (bf16[128,1536]{1,0:T(8,128)(2,1)S(1)}, bf16[128,1536]{1,0:T(8,128)(2,1)}, u32[]{:S(2)}, u32[]{:S(2)}) collective-permute-start(bf16[128,1536]{1,0:T(8,128)(2,1)S(1)} %add_convert_fusion.5.refs_10_.refs_1_), channel_id=1, source_target_pairs={{0,4},{4,0},{1,5},{5,1},{2,6},{6,2},{3,7},{7,3}} | collective-permute-start | bytes 1179656 | tf_op jit(solution)/shard_map/ppermute | solution.py:398
  332.1 31.0 %collective-permute-start.21 = (f32[192,1536]{1,0:T(8,128)}, f32[192,1536]{1,0:T(8,128)}, u32[]{:S(2)}, u32[]{:S(2)}) collective-permute-start(f32[192,1536]{1,0:T(8,128)} %get-tuple-element.80), channel_id=1, source_target_pairs={{0,4},{4,0},{1,5},{5,1},{2,6},{6,2},{3,7},{7,3}} | collective-permute-start | bytes 3538952 | tf_op jit(solution)/shard_map/ppermute | solution.py:398
  361.7 51.3 %collective-permute-start.23 = (f32[192,1536]{1,0:T(8,128)}, f32[192,1536]{1,0:T(8,128)}, u32[]{:S(2)}, u32[]{:S(2)}) collective-permute-start(f32[192,1536]{1,0:T(8,128)} %get-tuple-element.83), channel_id=1, source_target_pairs={{0,4},{4,0},{1,5},{5,1},{2,6},{6,2},{3,7},{7,3}} | collective-permute-start | bytes 3538952 | tf_op jit(solution)/shard_map/ppermute | solution.py:398
  365.1 37.1 %collective-permute-start.22 = (bf16[192,1536]{1,0:T(8,128)(2,1)S(1)}, bf16[192,1536]{1,0:T(8,128)(2,1)}, u32[]{:S(2)}, u32[]{:S(2)}) collective-permute-start(bf16[192,1536]{1,0:T(8,128)(2,1)S(1)} %add_convert_fusion.1.refs_1_), channel_id=1, source_target_pairs={{0,4},{4,0},{1,5},{5,1},{2,6},{6,2},{3,7},{7,3}} | collective-permute-start | bytes 1769480 | tf_op jit(solution)/shard_map/ppermute | solution.py:398
  415.2 14.2 %collective-permute-start.24 = (bf16[192,1536]{1,0:T(8,128)(2,1)S(1)}, bf16[192,1536]{1,0:T(8,128)(2,1)}, u32[]{:S(2)}, u32[]{:S(2)}) collective-permute-start(bf16[192,1536]{1,0:T(8,128)(2,1)S(1)} %add_convert_fusion.refs_1_), channel_id=1, source_target_pairs={{0,4},{4,0},{1,5},{5,1},{2,6},{6,2},{3,7},{7,3}} | collective-permute-start | bytes 1769480 | tf_op jit(solution)/shard_map/ppermute | solution.py:398
  441.6 3.8 collective-permute-start.25
  (22 other events, 67.8 us)
Sparse Core Ops, SparseCore 0:
  41.2 22.0 all-gather.3
  107.5 26.0 all-gather.7
  163.7 21.5 all-gather.5

commit v3 on v2

--- a/solution.py
+++ b/solution.py
@@ -70,7 +70,7 @@
     if at is not None:
         return [x[at:at + half] for x in xs]
     model = lax.axis_index('model')
-    pick = lambda side: [x[pl.ds(pl.multiple_of(side * (x.shape[0] // 2), 64), x.shape[0] // 2)] for x in xs]
+    pick = lambda side: [x[pl.ds(pl.multiple_of(side * (x.shape[0] // 2), 16), x.shape[0] // 2)] for x in xs]
     return [jnp.concatenate(pick(side)) for side in (1 - model, model)]
 
 
@@ -492,6 +492,8 @@
                 if c < end:
                     send(c)
             if c == 1:
+                tgt = tgt_own[0] - model_idx * w_head.shape[1]
+                tgt = held(jnp.concatenate([h for at, n in zip(starts, sizes) for h in halves(tgt, at, n)]), *tail)[:, None]
                 wo_far.append(joined(held(wo_sent[1], *tail)))
         gain = attn_norm[1][None]
         both_w = [w_next, w_far]
@@ -513,22 +515,16 @@
 
         mixes = {}
         for c in range(1, n_chunks):
-            mix = attention(c, both_w if c < end else both_w[:1], tail)
-            mixes[c] = [mix] if c < end else [mix, across(mix)]
+            mix = attention(c, both_w[:1], tail)
+            mixes[c] = [mix, across(mix)]
             tail = (mix,)
         for c in range(1, n_chunks):
-            if c < end:
-                tail = (*tail, collect(c - 1, *tail))
             tail = (mlp_of(1, c, wo_far[1], tail, mix=mixes[c]),)
-            if c == end:
-                collect(c - 1, *tail)
             send(c)
-        tgt = tgt_own[0] - model_idx * w_head.shape[1]
-        tgt = held(jnp.concatenate([h for at, n in zip(starts, sizes) for h in halves(tgt, at, n)]), *tail)[:, None]
+        for c in range(n_chunks):
+            tail = (*tail, collect(c, *tail))
         stats = []
         for c in range(n_chunks):
-            if c == end:
-                collect(c, *tail)
             out = head_chunk(*x_r[c], final_norm[None], w_head, tgt, starts[c], tail)
             tail = (out,)
             stats.append(jnp.concatenate(halves(out[:, :3], 0, sizes[c])))

time: 459 us -> 445 us (0.969)
  Pallas kernels: 270 us -> 262 us
  waiting for transfers between devices: 101 us -> 96.1 us
    pallas_call x16, Pallas kernels: 270 us -> 262 us  [call(): pl.pallas_call(run, grid=grid, in_specs=list(in_specs) + [ORDER_ONLY] * n...]
    ppermute x20 -> x21, waiting for transfers between devices: 97.1 us -> 91.7 us  [across(): return lax.ppermute(x, 'model', [(0, 1), (1, 0)])]
    ppermute x20 -> x21, starting transfers between devices: 20.8 us -> 21.1 us  [across(): return lax.ppermute(x, 'model', [(0, 1), (1, 0)])]
  transfers between devices with their start and end apart: 29 -> 30, of which waited for: 13 -> 17; matrix products, arithmetic and copies ran while one was open for 5% -> 5% of each run, Pallas kernels for 56% -> 56%
where the time goes in v3:
time: 445 us; the launch traced here: 439 us
  Pallas kernels  262 us (59%)
  waiting for transfers between devices  96.1 us (22%)
  starting transfers between devices  27.8 us (6%)
  local copies, waits for them, and re-layouts  23.6 us (5%)
  other arithmetic  15.5 us (3%)
  between operations  13.9 us (3%)
    pallas_call x16, Pallas kernels, call(): pl.pallas_call(run, grid=grid, in_specs=list(in_specs) + [ORDER_ONLY] * n...  262 us
    ppermute x21, waiting for transfers between devices, across(): return lax.ppermute(x, 'model', [(0, 1), (1, 0)])  91.7 us
    ppermute x21, starting transfers between devices, across(): return lax.ppermute(x, 'model', [(0, 1), (1, 0)])  21.1 us
    convert_element_type x6, other arithmetic, collect(): mine = (xm.astype(f32) + (keep + held(far.pop(c), *after))).astype(bf16)  11.3 us
  transfers between devices with their start and end apart: 30, of which 17 were waited for; matrix products, arithmetic and copies ran while one was open for 5% of the time, Pallas kernels for 56%

profile of v3, /device:TPU:0, one launch (start us, length us, event | category | flops | bytes accessed | tf_op | source)
XLA Modules:
  0.0 438.9 jit_solution(9025321639305317735)
XLA Ops:
  8.7 3.3 slice_bitcast_fusion.refs_4_
  14.5 2.7 dynamic-slice_bitcast_fusion
  17.2 3.5 shard_map.136.refs_11_
  20.7 3.3 collective-permute-start
  30.3 10.7 %shard_map.137 = (bf16[384,768]{1,0:T(8,128)(2,1)}, bf16[256,256]{1,0:T(8,128)(2,1)}) custom-call(bf16[1024,1536]{1,0:T(8,128)(2,1)} %bitcast.57, f32[1,1536]{1,0:T(1,128)} %get-tuple-element.102.refs_1_, f32[2,192,128]{2,1,0:T(8,128)} %pad_maximum_fusion.refs_2_.refs_3_.refs_9_, f32[2,8,128]{2,1,0:T(8,128)} %pad_maximum_fusion.1.refs_3_.refs_4_.refs_10_, ...), custom_call_target="tpu_custom_call" | custom-call | flops 1811939328 | tf_op jit(solution)/shard_map/pallas_call | solution.py:44
  41.3 3.9 slice_bitcast_fusion.2
  49.3 11.5 %shard_map.138 = (bf16[384,768]{1,0:T(8,128)(2,1)}, bf16[384,256]{1,0:T(8,128)(2,1)}) custom-call(bf16[1024,1536]{1,0:T(8,128)(2,1)} %bitcast.58, f32[1,1536]{1,0:T(1,128)} %get-tuple-element.102.refs_1_, f32[2,192,128]{2,1,0:T(8,128)} %pad_maximum_fusion.refs_2_.refs_3_.refs_9_, f32[2,8,128]{2,1,0:T(8,128)} %pad_maximum_fusion.1.refs_3_.refs_4_.refs_10_, ...), custom_call_target="tpu_custom_call" | custom-call | flops 3623878656 | tf_op jit(solution)/shard_map/pallas_call | solution.py:44
  60.8 12.1 %shard_map.139 = (bf16[384,768]{1,0:T(8,128)(2,1)}, bf16[384,256]{1,0:T(8,128)(2,1)}) custom-call(bf16[1024,1536]{1,0:T(8,128)(2,1)} %bitcast.59, f32[1,1536]{1,0:T(1,128)} %get-tuple-element.102.refs_1_, f32[2,192,128]{2,1,0:T(8,128)} %pad_maximum_fusion.refs_2_.refs_3_.refs_9_, f32[2,8,128]{2,1,0:T(8,128)} %pad_maximum_fusion.1.refs_3_.refs_4_.refs_10_, ...), custom_call_target="tpu_custom_call" | custom-call | flops 4529848320 | tf_op jit(solution)/shard_map/pallas_call | solution.py:44
  72.9 6.9 %collective-permute-done.4.refs_9_ = bf16[384,768]{1,0:T(8,128)(2,1)} collective-permute-done((bf16[384,768]{1,0:T(8,128)(2,1)}, bf16[384,768]{1,0:T(8,128)(2,1)}, u32[]{:S(2)}, u32[]{:S(2)}) %collective-permute-start.4) | collective-permute-done | bytes 589856 | tf_op jit(solution)/shard_map/ppermute | solution.py:398
  79.8 26.3 %shard_map.140 = (f32[192,1536]{1,0:T(8,128)}, f32[192,1536]{1,0:T(8,128)}, bf16[192,1536]{1,0:T(8,128)(2,1)}) custom-call(bf16[128,1536]{1,0:T(8,128)(2,1)} %refs_0_.3, bf16[1024,1536]{1,0:T(8,128)(2,1)} %bitcast.60, f32[1,1536]{1,0:T(1,128)} %get-tuple-element.104.refs_2_.refs_1_, bf16[2,768,1536]{2,1,0:T(8,128)(2,1)} %bitcast.51, ...), custom_call_target="tpu_custom_call" | custom-call | flops 15854469120 | tf_op jit(solution)/shard_map/pallas_call | solution.py:44
  110.1 13.7 %collective-permute-done.6.refs_8_ = bf16[384,768]{1,0:T(8,128)(2,1)S(1)} collective-permute-done((bf16[384,768]{1,0:T(8,128)(2,1)}, bf16[384,768]{1,0:T(8,128)(2,1)S(1)}, u32[]{:S(2)}, u32[]{:S(2)}) %collective-permute-start.6) | collective-permute-done | bytes 589856 | tf_op jit(solution)/shard_map/ppermute | solution.py:398
  124.6 26.3 %shard_map.141 = (f32[192,1536]{1,0:T(8,128)}, f32[192,1536]{1,0:T(8,128)}, bf16[192,1536]{1,0:T(8,128)(2,1)}) custom-call(bf16[1024,1536]{1,0:T(8,128)(2,1)} %bitcast.61, f32[1,1536]{1,0:T(1,128)} %get-tuple-element.104.refs_2_.refs_1_, bf16[2,768,1536]{2,1,0:T(8,128)(2,1)} %bitcast.52, bf16[768,1536]{1,0:T(8,128)(2,1)} %all-gather.4.cloned.1.call-done.refs_4_.refs_3_, ...), custom_call_target="tpu_custom_call" | custom-call | flops 15854469120 | tf_op jit(solution)/shard_map/pallas_call | solution.py:44
  150.9 10.0 %collective-permute-done.5 = f32[192,1536]{1,0:T(8,128)} collective-permute-done((f32[192,1536]{1,0:T(8,128)}, f32[192,1536]{1,0:T(8,128)}, u32[]{:S(2)}, u32[]{:S(2)}) %collective-permute-start.5) | collective-permute-done | bytes 1179680 | tf_op jit(solution)/shard_map/ppermute | solution.py:398
  160.9 2.1 add_convert_fusion.4.refs_10_.refs_1_
  165.8 13.6 %collective-permute-done.10.refs_8_ = bf16[384,768]{1,0:T(8,128)(2,1)} collective-permute-done((bf16[384,768]{1,0:T(8,128)(2,1)S(1)}, bf16[384,768]{1,0:T(8,128)(2,1)}, u32[]{:S(2)}, u32[]{:S(2)}) %collective-permute-start.10) | collective-permute-done | bytes 589856 | tf_op jit(solution)/shard_map/ppermute | solution.py:398
  179.4 26.3 %shard_map.142 = (f32[192,1536]{1,0:T(8,128)}, f32[192,1536]{1,0:T(8,128)}, bf16[192,1536]{1,0:T(8,128)(2,1)}) custom-call(bf16[1024,1536]{1,0:T(8,128)(2,1)} %bitcast.62, f32[1,1536]{1,0:T(1,128)} %get-tuple-element.104.refs_2_.refs_1_, bf16[2,768,1536]{2,1,0:T(8,128)(2,1)} %bitcast.53, bf16[768,1536]{1,0:T(8,128)(2,1)} %all-gather.4.cloned.1.call-done.refs_4_.refs_3_, ...), custom_call_target="tpu_custom_call" | custom-call | flops 15854469120 | tf_op jit(solution)/shard_map/pallas_call | solution.py:44
  206.4 10.9 %collective-permute-done.7.refs_0_ = bf16[192,1536]{1,0:T(8,128)(2,1)} collective-permute-done((bf16[192,1536]{1,0:T(8,128)(2,1)S(1)}, bf16[192,1536]{1,0:T(8,128)(2,1)}, u32[]{:S(2)}, u32[]{:S(2)}) %collective-permute-start.7) | collective-permute-done | bytes 589856 | tf_op jit(solution)/shard_map/ppermute | solution.py:398
  217.3 4.4 %shard_map.143.refs_17_.refs_21_.refs_8_ = bf16[128,512]{1,0:T(8,128)(2,1)} custom-call(bf16[192,1536]{1,0:T(8,128)(2,1)} %collective-permute-done.7.refs_0_, bf16[192,1536]{1,0:T(8,128)(2,1)} %copy-done, f32[1,1536]{1,0:T(1,128)} %get-tuple-element.101.refs_2_.refs_8_, f32[2,192,128]{2,1,0:T(8,128)} %pad_maximum_fusion.refs_2_.refs_3_.refs_9_, ...), custom_call_target="tpu_custom_call" | custom-call | flops 402653184 | tf_op jit(solution)/shard_map/pallas_call | solution.py:44
  225.0 2.0 add_convert_fusion.3.refs_22_.refs_1_
  230.6 33.5 %shard_map.144 = (f32[128,1536]{1,0:T(8,128)}, f32[128,1536]{1,0:T(8,128)}, bf16[128,1536]{1,0:T(8,128)(2,1)}, bf16[256,512]{1,0:T(8,128)(2,1)}) custom-call(bf16[192,1536]{1,0:T(8,128)(2,1)} %collective-permute-done.7.refs_0_, bf16[192,1536]{1,0:T(8,128)(2,1)} %copy-done, f32[1,1536]{1,0:T(1,128)} %get-tuple-element.103.refs_2_, ...), custom_call_target="tpu_custom_call" | custom-call | flops 14092861440 | tf_op jit(solution)/shard_map/pallas_call | solution.py:44
  264.1 2.9 add_convert_fusion.2.refs_14_.refs_1_
  267.5 11.7 %shard_map.145 = (bf16[384,768]{1,0:T(8,128)(2,1)}, bf16[384,256]{1,0:T(8,128)(2,1)}) custom-call(bf16[192,1536]{1,0:T(8,128)(2,1)} %collective-permute-done.18.refs_0_, bf16[192,1536]{1,0:T(8,128)(2,1)} %copy-done.3, f32[1,1536]{1,0:T(1,128)} %get-tuple-element.101.refs_2_.refs_8_, f32[2,192,128]{2,1,0:T(8,128)} %pad_maximum_fusion.refs_2_.refs_3_.refs_9_, ...), custom_call_target="tpu_custom_call" | custom-call | flops 3623878656 | tf_op jit(solution)/shard_map/pallas_call | solution.py:44
  283.5 11.9 %shard_map.146 = (bf16[384,768]{1,0:T(8,128)(2,1)}, bf16[384,256]{1,0:T(8,128)(2,1)}) custom-call(bf16[192,1536]{1,0:T(8,128)(2,1)} %collective-permute-done.17.refs_0_, bf16[192,1536]{1,0:T(8,128)(2,1)} %add_convert_fusion.2.refs_14_.refs_1_, f32[1,1536]{1,0:T(1,128)} %get-tuple-element.101.refs_2_.refs_8_, ...), custom_call_target="tpu_custom_call" | custom-call | flops 4529848320 | tf_op jit(solution)/shard_map/pallas_call | solution.py:44
  296.2 26.3 %shard_map.147 = (f32[192,1536]{1,0:T(8,128)}, f32[192,1536]{1,0:T(8,128)}, bf16[192,1536]{1,0:T(8,128)(2,1)}) custom-call(bf16[192,1536]{1,0:T(8,128)(2,1)} %collective-permute-done.18.refs_0_, bf16[192,1536]{1,0:T(8,128)(2,1)} %copy-done.3, f32[1,1536]{1,0:T(1,128)} %get-tuple-element.103.refs_2_, bf16[2,768,1536]{2,1,0:T(8,128)(2,1)} %bitcast.55, ...), custom_call_target="tpu_custom_call" | custom-call | flops 15854469120 | tf_op jit(solution)/shard_map/pallas_call | solution.py:44
  326.4 26.4 %shard_map.148 = (f32[192,1536]{1,0:T(8,128)}, f32[192,1536]{1,0:T(8,128)}, bf16[192,1536]{1,0:T(8,128)(2,1)}) custom-call(bf16[192,1536]{1,0:T(8,128)(2,1)} %collective-permute-done.17.refs_0_, bf16[192,1536]{1,0:T(8,128)(2,1)} %add_convert_fusion.2.refs_14_.refs_1_, f32[1,1536]{1,0:T(1,128)} %get-tuple-element.103.refs_2_, bf16[2,768,1536]{2,1,0:T(8,128)(2,1)} %bitcast.56, ...), custom_call_target="tpu_custom_call" | custom-call | flops 15854469120 | tf_op jit(solution)/shard_map/pallas_call | solution.py:44
  357.6 2.5 add_convert_fusion.1.refs_7_.refs_1_
  360.9 21.0 %collective-permute-done.23 = f32[192,1536]{1,0:T(8,128)S(1)} collective-permute-done((f32[192,1536]{1,0:T(8,128)}, f32[192,1536]{1,0:T(8,128)S(1)}, u32[]{:S(2)}, u32[]{:S(2)}) %collective-permute-start.23) | collective-permute-done | bytes 1179680 | tf_op jit(solution)/shard_map/ppermute | solution.py:398
  383.0 7.3 %collective-permute-done.21.refs_0_ = bf16[128,1536]{1,0:T(8,128)(2,1)S(1)} collective-permute-done((bf16[128,1536]{1,0:T(8,128)(2,1)S(1)}, bf16[128,1536]{1,0:T(8,128)(2,1)S(1)}, u32[]{:S(2)}, u32[]{:S(2)}) %collective-permute-start.21) | collective-permute-done | bytes 393248 | tf_op jit(solution)/shard_map/ppermute | solution.py:398
  391.1 9.1 %shard_map.149.refs_5_ = f32[256,128]{1,0:T(8,128)} custom-call(bf16[128,1536]{1,0:T(8,128)(2,1)} %copy-done.27, bf16[128,1536]{1,0:T(8,128)(2,1)} %copy-done.16, f32[1,1536]{1,0:T(1,128)} %broadcast_in_dim.10.refs_2_, bf16[1536,4096]{1,0:T(8,128)(2,1)} %refs_3_.5, s32[1024,1]{1,0:T(8,128)} %copy.20.refs_4_, f32[192,1536]{1,0:T(8,128)} %get-tuple-element.76.refs_5_, ...), custom_call_target="tpu_custom_call" | custom-call | flops 6442450944 | tf_op jit(solution)/shard_map/pallas_call | solution.py:44
  403.1 10.8 %shard_map.150.refs_5_ = f32[384,128]{1,0:T(8,128)} custom-call(bf16[192,1536]{1,0:T(8,128)(2,1)} %collective-permute-done.24.refs_0_, bf16[192,1536]{1,0:T(8,128)(2,1)} %add_convert_fusion.1.refs_7_.refs_1_, f32[1,1536]{1,0:T(1,128)} %broadcast_in_dim.10.refs_2_, bf16[1536,4096]{1,0:T(8,128)(2,1)} %refs_3_.5, s32[1024,1]{1,0:T(8,128)} %copy.20.refs_4_, ...), custom_call_target="tpu_custom_call" | custom-call | flops 9663676416 | tf_op jit(solution)/shard_map/pallas_call | solution.py:44
  415.0 11.2 %shard_map.151 = f32[384,128]{1,0:T(8,128)} custom-call(bf16[192,1536]{1,0:T(8,128)(2,1)} %collective-permute-done.25.refs_0_, bf16[192,1536]{1,0:T(8,128)(2,1)} %copy-done.14, f32[1,1536]{1,0:T(1,128)} %broadcast_in_dim.10.refs_2_, bf16[1536,4096]{1,0:T(8,128)(2,1)} %refs_3_.5, s32[1024,1]{1,0:T(8,128)} %copy.20.refs_4_, f32[384,128]{1,0:T(8,128)} %shard_map.150.refs_5_), custom_call_target="tpu_custom_call" | custom-call | flops 9663676416 | tf_op jit(solution)/shard_map/pallas_call | solution.py:44
  428.3 2.9 collective-permute-done.26
  (145 shorter events, 53.8 us)
Async XLA Ops:
  6.5 73.3 %all-gather.4.cloned.1.call-start = ((), (), s32[]{:S(2)}) async-start(), calls=%async_computation | async-start | bytes 2949120 | tf_op jit(solution)/shard_map/all_gather | solution.py:413
  14.5 30.8 %copy-start.1 = (bf16[1,1536,128]{2,1,0:T(8,128)(2,1)}, bf16[1,1536,128]{2,1,0:T(8,128)(2,1)S(1)}, u32[]{:S(2)}) copy-start(bf16[1,1536,128]{2,1,0:T(8,128)(2,1)S(1)} %get-tuple-element.91.refs_7_.refs_13_) | copy-start | bytes 1179652
  14.5 30.8 %copy-start.2 = (bf16[1,1536,128]{2,1,0:T(8,128)(2,1)}, bf16[1,1536,128]{2,1,0:T(8,128)(2,1)S(1)}, u32[]{:S(2)}) copy-start(bf16[1,1536,128]{2,1,0:T(8,128)(2,1)S(1)} %get-tuple-element.125.refs_6_.refs_12_) | copy-start | bytes 1179652
  20.7 20.4 %collective-permute-start = (bf16[192,1536]{1,0:T(8,128)(2,1)}, bf16[192,1536]{1,0:T(8,128)(2,1)}, u32[]{:S(2)}, u32[]{:S(2)}) collective-permute-start(bf16[192,1536]{1,0:T(8,128)(2,1)} %get-tuple-element.45), channel_id=1, source_target_pairs={{0,4},{4,0},{1,5},{5,1},{2,6},{6,2},{3,7},{7,3}} | collective-permute-start | bytes 1769480 | tf_op jit(solution)/shard_map/ppermute | solution.py:398
  24.8 3.8 collective-permute-start.1
  24.9 4.6 %collective-permute-start.2 = (bf16[128,256]{1,0:T(8,128)(2,1)S(1)}, bf16[128,256]{1,0:T(8,128)(2,1)S(1)}, u32[]{:S(2)}, u32[]{:S(2)}) collective-permute-start(bf16[128,256]{1,0:T(8,128)(2,1)S(1)} %slice.87.refs_7_), channel_id=1, source_target_pairs={{0,2},{1,3},{2,0},{3,1},{4,6},{5,7},{6,4},{7,5}} | collective-permute-start | bytes 196616 | tf_op jit(solution)/shard_map/ppermute | solution.py:401
  26.4 3.3 collective-permute-start.3
  41.1 176.2 %all-gather.8.cloned.1.call-start = ((), (), s32[]{:S(2)}) async-start(), calls=%async_computation.2 | async-start | bytes 3932160 | tf_op jit(solution)/shard_map/all_gather | solution.py:413
  46.7 59.5 %collective-permute-start.9 = (bf16[2,1536,128]{2,1,0:T(8,128)(2,1)}, bf16[2,1536,128]{2,1,0:T(8,128)(2,1)S(1)}, u32[]{:S(2)}, u32[]{:S(2)}) collective-permute-start(bf16[2,1536,128]{2,1,0:T(8,128)(2,1)} %fusion.1), channel_id=1, source_target_pairs={{0,4},{4,0},{1,5},{5,1},{2,6},{6,2},{3,7},{7,3}} | collective-permute-start | bytes 2359304 | tf_op jit(solution)/shard_map/ppermute | solution.py:398
  47.8 32.0 %collective-permute-start.4 = (bf16[384,768]{1,0:T(8,128)(2,1)}, bf16[384,768]{1,0:T(8,128)(2,1)}, u32[]{:S(2)}, u32[]{:S(2)}) collective-permute-start(bf16[384,768]{1,0:T(8,128)(2,1)} %get-tuple-element.46.refs_12_.refs_8_), channel_id=1, source_target_pairs={{0,4},{4,0},{1,5},{5,1},{2,6},{6,2},{3,7},{7,3}} | collective-permute-start | bytes 1769480 | tf_op jit(solution)/shard_map/ppermute | solution.py:398
  107.1 120.5 %all-gather.6.cloned.1.call-start = ((), (), s32[]{:S(2)}) async-start(), calls=%async_computation.1 | async-start | bytes 2949120 | tf_op jit(solution)/shard_map/all_gather | solution.py:413
  107.3 16.4 %collective-permute-start.6 = (bf16[384,768]{1,0:T(8,128)(2,1)}, bf16[384,768]{1,0:T(8,128)(2,1)S(1)}, u32[]{:S(2)}, u32[]{:S(2)}) collective-permute-start(bf16[384,768]{1,0:T(8,128)(2,1)} %get-tuple-element.50.refs_13_.refs_7_), channel_id=1, source_target_pairs={{0,4},{4,0},{1,5},{5,1},{2,6},{6,2},{3,7},{7,3}} | collective-permute-start | bytes 1769480 | tf_op jit(solution)/shard_map/ppermute | solution.py:398
  108.0 55.0 %collective-permute-start.8 = (bf16[192,1536]{1,0:T(8,128)(2,1)}, bf16[192,1536]{1,0:T(8,128)(2,1)}, u32[]{:S(2)}, u32[]{:S(2)}) collective-permute-start(bf16[192,1536]{1,0:T(8,128)(2,1)} %get-tuple-element.57), channel_id=1, source_target_pairs={{0,4},{4,0},{1,5},{5,1},{2,6},{6,2},{3,7},{7,3}} | collective-permute-start | bytes 1769480 | tf_op jit(solution)/shard_map/ppermute | solution.py:398
  109.3 51.6 %collective-permute-start.5 = (f32[192,1536]{1,0:T(8,128)}, f32[192,1536]{1,0:T(8,128)}, u32[]{:S(2)}, u32[]{:S(2)}) collective-permute-start(f32[192,1536]{1,0:T(8,128)} %get-tuple-element.54), channel_id=1, source_target_pairs={{0,4},{4,0},{1,5},{5,1},{2,6},{6,2},{3,7},{7,3}} | collective-permute-start | bytes 3538952 | tf_op jit(solution)/shard_map/ppermute | solution.py:398
  163.0 16.3 %collective-permute-start.10 = (bf16[384,768]{1,0:T(8,128)(2,1)S(1)}, bf16[384,768]{1,0:T(8,128)(2,1)}, u32[]{:S(2)}, u32[]{:S(2)}) collective-permute-start(bf16[384,768]{1,0:T(8,128)(2,1)S(1)} %copy-done.5), channel_id=1, source_target_pairs={{0,4},{4,0},{1,5},{5,1},{2,6},{6,2},{3,7},{7,3}} | collective-permute-start | bytes 1769480 | tf_op jit(solution)/shard_map/ppermute | solution.py:398
  163.8 61.2 %collective-permute-start.14 = (f32[192,1536]{1,0:T(8,128)}, f32[192,1536]{1,0:T(8,128)}, u32[]{:S(2)}, u32[]{:S(2)}) collective-permute-start(f32[192,1536]{1,0:T(8,128)} %get-tuple-element.63), channel_id=1, source_target_pairs={{0,4},{4,0},{1,5},{5,1},{2,6},{6,2},{3,7},{7,3}} | collective-permute-start | bytes 3538952 | tf_op jit(solution)/shard_map/ppermute | solution.py:398
  165.1 52.2 %collective-permute-start.7 = (bf16[192,1536]{1,0:T(8,128)(2,1)S(1)}, bf16[192,1536]{1,0:T(8,128)(2,1)}, u32[]{:S(2)}, u32[]{:S(2)}) collective-permute-start(bf16[192,1536]{1,0:T(8,128)(2,1)S(1)} %add_convert_fusion.4.refs_10_.refs_1_), channel_id=1, source_target_pairs={{0,4},{4,0},{1,5},{5,1},{2,6},{6,2},{3,7},{7,3}} | collective-permute-start | bytes 1769480 | tf_op jit(solution)/shard_map/ppermute | solution.py:398
  205.7 58.4 %collective-permute-start.16 = (f32[192,1536]{1,0:T(8,128)}, f32[192,1536]{1,0:T(8,128)}, u32[]{:S(2)}, u32[]{:S(2)}) collective-permute-start(f32[192,1536]{1,0:T(8,128)} %get-tuple-element.69), channel_id=1, source_target_pairs={{0,4},{4,0},{1,5},{5,1},{2,6},{6,2},{3,7},{7,3}} | collective-permute-start | bytes 3538952 | tf_op jit(solution)/shard_map/ppermute | solution.py:398
  221.7 5.9 %collective-permute-start.11 = (bf16[128,512]{1,0:T(8,128)(2,1)}, bf16[128,512]{1,0:T(8,128)(2,1)S(1)}, u32[]{:S(2)}, u32[]{:S(2)}) collective-permute-start(bf16[128,512]{1,0:T(8,128)(2,1)} %shard_map.143.refs_17_.refs_21_.refs_8_), channel_id=1, source_target_pairs={{0,1},{1,2},{2,3},{3,0},{4,5},{5,6},{6,7},{7,4}} | collective-permute-start | bytes 393224 | tf_op jit(solution)/shard_map/ppermute | solution.py:401
  221.7 6.6 %collective-permute-start.12 = (bf16[128,512]{1,0:T(8,128)(2,1)}, bf16[128,512]{1,0:T(8,128)(2,1)S(1)}, u32[]{:S(2)}, u32[]{:S(2)}) collective-permute-start(bf16[128,512]{1,0:T(8,128)(2,1)} %shard_map.143.refs_17_.refs_21_.refs_8_), channel_id=1, source_target_pairs={{0,2},{1,3},{2,0},{3,1},{4,6},{5,7},{6,4},{7,5}} | collective-permute-start | bytes 393224 | tf_op jit(solution)/shard_map/ppermute | solution.py:401
  223.5 6.4 %collective-permute-start.13 = (bf16[128,512]{1,0:T(8,128)(2,1)}, bf16[128,512]{1,0:T(8,128)(2,1)S(1)}, u32[]{:S(2)}, u32[]{:S(2)}) collective-permute-start(bf16[128,512]{1,0:T(8,128)(2,1)} %shard_map.143.refs_17_.refs_21_.refs_8_), channel_id=1, source_target_pairs={{0,3},{1,0},{2,1},{3,2},{4,7},{5,4},{6,5},{7,6}} | collective-permute-start | bytes 393224 | tf_op jit(solution)/shard_map/ppermute | solution.py:401
  227.0 40.5 %collective-permute-start.18 = (bf16[192,1536]{1,0:T(8,128)(2,1)S(1)}, bf16[192,1536]{1,0:T(8,128)(2,1)}, u32[]{:S(2)}, u32[]{:S(2)}) collective-permute-start(bf16[192,1536]{1,0:T(8,128)(2,1)S(1)} %add_convert_fusion.3.refs_22_.refs_1_), channel_id=1, source_target_pairs={{0,4},{4,0},{1,5},{5,1},{2,6},{6,2},{3,7},{7,3}} | collective-permute-start | bytes 1769480 | tf_op jit(solution)/shard_map/ppermute | solution.py:398
  267.0 16.5 %collective-permute-start.17 = (bf16[192,1536]{1,0:T(8,128)(2,1)}, bf16[192,1536]{1,0:T(8,128)(2,1)}, u32[]{:S(2)}, u32[]{:S(2)}) collective-permute-start(bf16[192,1536]{1,0:T(8,128)(2,1)} %add_convert_fusion.2.refs_14_.refs_1_), channel_id=1, source_target_pairs={{0,4},{4,0},{1,5},{5,1},{2,6},{6,2},{3,7},{7,3}} | collective-permute-start | bytes 1769480 | tf_op jit(solution)/shard_map/ppermute | solution.py:398
  279.3 16.9 %collective-permute-start.20 = (bf16[384,768]{1,0:T(8,128)(2,1)}, bf16[384,768]{1,0:T(8,128)(2,1)}, u32[]{:S(2)}, u32[]{:S(2)}) collective-permute-start(bf16[384,768]{1,0:T(8,128)(2,1)} %get-tuple-element.73.refs_14_.refs_8_), channel_id=1, source_target_pairs={{0,4},{4,0},{1,5},{5,1},{2,6},{6,2},{3,7},{7,3}} | collective-permute-start | bytes 1769480 | tf_op jit(solution)/shard_map/ppermute | solution.py:398
  281.5 73.3 %collective-permute-start.15 = (f32[128,1536]{1,0:T(8,128)}, f32[128,1536]{1,0:T(8,128)}, u32[]{:S(2)}, u32[]{:S(2)}) collective-permute-start(f32[128,1536]{1,0:T(8,128)} %get-tuple-element.67), channel_id=1, source_target_pairs={{0,4},{4,0},{1,5},{5,1},{2,6},{6,2},{3,7},{7,3}} | collective-permute-start | bytes 2359304 | tf_op jit(solution)/shard_map/ppermute | solution.py:398
  295.5 30.1 %collective-permute-start.19 = (bf16[384,768]{1,0:T(8,128)(2,1)}, bf16[384,768]{1,0:T(8,128)(2,1)S(1)}, u32[]{:S(2)}, u32[]{:S(2)}) collective-permute-start(bf16[384,768]{1,0:T(8,128)(2,1)} %get-tuple-element.74.refs_10_.refs_8_), channel_id=1, source_target_pairs={{0,4},{4,0},{1,5},{5,1},{2,6},{6,2},{3,7},{7,3}} | collective-permute-start | bytes 1769480 | tf_op jit(solution)/shard_map/ppermute | solution.py:398
  322.4 35.1 %collective-permute-start.22 = (f32[192,1536]{1,0:T(8,128)}, f32[192,1536]{1,0:T(8,128)}, u32[]{:S(2)}, u32[]{:S(2)}) collective-permute-start(f32[192,1536]{1,0:T(8,128)} %get-tuple-element.80), channel_id=1, source_target_pairs={{0,4},{4,0},{1,5},{5,1},{2,6},{6,2},{3,7},{7,3}} | collective-permute-start | bytes 3538952 | tf_op jit(solution)/shard_map/ppermute | solution.py:398
  352.9 29.1 %collective-permute-start.23 = (f32[192,1536]{1,0:T(8,128)}, f32[192,1536]{1,0:T(8,128)S(1)}, u32[]{:S(2)}, u32[]{:S(2)}) collective-permute-start(f32[192,1536]{1,0:T(8,128)} %get-tuple-element.83), channel_id=1, source_target_pairs={{0,4},{4,0},{1,5},{5,1},{2,6},{6,2},{3,7},{7,3}} | collective-permute-start | bytes 3538952 | tf_op jit(solution)/shard_map/ppermute | solution.py:398
  356.3 34.1 %collective-permute-start.21 = (bf16[128,1536]{1,0:T(8,128)(2,1)S(1)}, bf16[128,1536]{1,0:T(8,128)(2,1)S(1)}, u32[]{:S(2)}, u32[]{:S(2)}) collective-permute-start(bf16[128,1536]{1,0:T(8,128)(2,1)S(1)} %add_convert_fusion.5.refs_1_.refs_6_), channel_id=1, source_target_pairs={{0,4},{4,0},{1,5},{5,1},{2,6},{6,2},{3,7},{7,3}} | collective-permute-start | bytes 1179656 | tf_op jit(solution)/shard_map/ppermute | solution.py:398
  360.1 43.0 %collective-permute-start.24 = (bf16[192,1536]{1,0:T(8,128)(2,1)}, bf16[192,1536]{1,0:T(8,128)(2,1)}, u32[]{:S(2)}, u32[]{:S(2)}) collective-permute-start(bf16[192,1536]{1,0:T(8,128)(2,1)} %add_convert_fusion.1.refs_7_.refs_1_), channel_id=1, source_target_pairs={{0,4},{4,0},{1,5},{5,1},{2,6},{6,2},{3,7},{7,3}} | collective-permute-start | bytes 1769480 | tf_op jit(solution)/shard_map/ppermute | solution.py:398
  382.2 32.8 %collective-permute-start.25 = (bf16[192,1536]{1,0:T(8,128)(2,1)S(1)}, bf16[192,1536]{1,0:T(8,128)(2,1)}, u32[]{:S(2)}, u32[]{:S(2)}) collective-permute-start(bf16[192,1536]{1,0:T(8,128)(2,1)S(1)} %add_convert_fusion.refs_8_.refs_1_), channel_id=1, source_target_pairs={{0,4},{4,0},{1,5},{5,1},{2,6},{6,2},{3,7},{7,3}} | collective-permute-start | bytes 1769480 | tf_op jit(solution)/shard_map/ppermute | solution.py:398
  427.5 3.8 collective-permute-start.26
  (26 other events, 167.5 us)
Sparse Core Ops, SparseCore 0:
  41.2 22.0 all-gather.3
  107.2 26.0 all-gather.7
  163.2 21.6 all-gather.5
